TPU v7x, 8 devices: a whole 2x2x1 slice. The times are simulated.
8 devices in a mesh: data: 1 (over z), dap2: 2 (over y), dap: 4 (over x, core).
Axes of the slice: x: 2, y: 2, z: 1, core: 2. Of those that a mesh axis runs over, the one named last changes fastest.
Arguments:
- pair_rep: bfloat16 [640, 640, 128], P(('data', 'dap2', 'dap'))
- pair_mask: int32 [640, 640], P(('data', 'dap2', 'dap'))
- norm_in: bfloat16 [6, 2, 2, 128], replicated
- norm_out: bfloat16 [6, 2, 2, 128], replicated
- w_ab: bfloat16 [6, 2, 128, 512], replicated
- w_gate: bfloat16 [6, 2, 128, 128], replicated
- w_out: bfloat16 [6, 2, 128, 128], replicated
Outputs:
- output: bfloat16 [640, 640, 128], P(('data', 'dap2', 'dap'))
All inputs are finite; a program needn't handle non-finite values.
Results may differ from a plain program's by a relative error of at most 0.0141214.
Values are sent between devices in bfloat16 or wider.
A program may use at most 1 GiB of HBM per device.

v0:
```python
import jax
import jax.numpy as jnp
from jax import lax
from jax.sharding import PartitionSpec as P

LN_EPS = 1e-5
ROW_AXES = ("dap2", "dap")
ALL_ROWS = ("data", "dap2", "dap")


def layer_norm(values, gain_vec, shift_vec, norm_axis):
    mean_val = jnp.mean(values, axis=norm_axis, keepdims=True)
    centered = values - mean_val
    var_val = jnp.mean(centered * centered, axis=norm_axis, keepdims=True)
    return centered * lax.rsqrt(var_val + LN_EPS) * gain_vec + shift_vec


def row_inputs(pair_loc, mask_loc, norm_in, w_ab):
    hidden = w_ab.shape[1] // 4
    pair_f = pair_loc.astype(jnp.float32)
    x_ln = layer_norm(pair_f, norm_in[0].astype(jnp.float32), norm_in[1].astype(jnp.float32), -1).astype(jnp.bfloat16)
    proj_all = jnp.einsum("de,ikd->eik", w_ab, x_ln, preferred_element_type=jnp.float32)
    proj_four = proj_all.reshape(2, 2, hidden, pair_loc.shape[0], pair_loc.shape[1])
    ab_rows = (mask_loc * jax.nn.sigmoid(proj_four[:, 1]) * proj_four[:, 0]).astype(jnp.bfloat16)
    return pair_f, x_ln, ab_rows


def finish_update(pair_f, x_ln, tri_rows, norm_out, w_gate, w_out):
    gain_vec = norm_out[0].astype(jnp.float32)[:, None, None]
    shift_vec = norm_out[1].astype(jnp.float32)[:, None, None]
    y_ln = layer_norm(tri_rows.astype(jnp.float32), gain_vec, shift_vec, 0).astype(jnp.bfloat16)
    update_val = jnp.einsum("cij,cd->ijd", y_ln, w_out, preferred_element_type=jnp.float32)
    gate_val = jax.nn.sigmoid(jnp.einsum("ijd,de->ije", x_ln, w_gate, preferred_element_type=jnp.float32))
    return (pair_f + gate_val * update_val).astype(jnp.bfloat16)


def tri_update(pair_loc, mask_loc, norm_in, norm_out, w_ab, w_gate, w_out, outgoing):
    pair_f, x_ln, ab_rows = row_inputs(pair_loc, mask_loc, norm_in, w_ab)
    ab_cols = lax.all_to_all(ab_rows, ROW_AXES, 1, 2, tiled=True)
    einsum_form = "cik,cjk->cij" if outgoing else "cki,ckj->cij"
    tri_full = jnp.einsum(einsum_form, ab_cols[0], ab_cols[1], preferred_element_type=jnp.float32).astype(jnp.bfloat16)
    tri_rows = lax.all_to_all(tri_full, ROW_AXES, 1, 0, tiled=True)
    return finish_update(pair_f, x_ln, tri_rows, norm_out, w_gate, w_out)


def solution(mesh):
    row_spec = P(ALL_ROWS, None, None)
    mask_spec = P(ALL_ROWS, None)

    def local_stack(pair_rep, pair_mask, norm_in, norm_out, w_ab, w_gate, w_out):
        mask_f = pair_mask.astype(jnp.float32)
        pair_cur = pair_rep
        for layer_idx in range(w_ab.shape[0]):
            for upd_idx in range(2):
                pair_cur = tri_update(pair_cur, mask_f, norm_in[layer_idx, upd_idx], norm_out[layer_idx, upd_idx], w_ab[layer_idx, upd_idx], w_gate[layer_idx, upd_idx], w_out[layer_idx, upd_idx], upd_idx == 0)
        return pair_cur

    return jax.shard_map(local_stack, mesh=mesh, in_specs=(row_spec, mask_spec, P(), P(), P(), P(), P()), out_specs=row_spec, check_vma=False)
```

profile of v0, /device:TPU:0, one launch (start us, length us, event | category | flops | bytes accessed | tf_op | source)
XLA Modules:
  0.0 9567.0 jit_solution(5424264401422107154)
XLA Ops:
  37.3 40.1 fusion.288
  77.5 69.4 fusion.396
  146.9 90.7 fusion.78
  237.7 294.2 %all_to_all.288 = bf16[2,128,80,640]{3,2,0,1:T(8,128)(2,1)} all-to-all(bf16[2,128,80,640]{3,2,0,1:T(8,128)(2,1)} %fusion.78), channel_id=1, replica_groups=mesh['data'=1,'dap2'=2,'dap'=4] {'dap2','dap'}, dimensions={1} | all-to-all | bytes 52428800 | tf_op jit(solution)/shard_map/all_to_all | solution.py:39
  637.0 129.3 %all-to-all-done.1 = bf16[16,640,640]{2,0,1:T(8,128)(2,1)} async-done(((bf16[16,640,640]{2,0,1:T(8,128)(2,1)}), bf16[16,640,640]{2,0,1:T(8,128)(2,1)}, u32[]{:S(2)}, u32[]{:S(2)}) %all-to-all-start.1) | async-done | bytes 13107232 | tf_op jit(solution)/shard_map/all_to_all | solution.py:42
  796.6 25.2 convert_reduce_fusion.10
  831.9 39.9 fusion.286
  871.8 69.4 fusion.395
  941.2 90.9 fusion.71
  1032.1 293.1 %all_to_all.289 = bf16[2,128,80,640]{3,2,0,1:T(8,128)(2,1)} all-to-all(bf16[2,128,80,640]{3,2,0,1:T(8,128)(2,1)} %fusion.71), channel_id=1, replica_groups=mesh['data'=1,'dap2'=2,'dap'=4] {'dap2','dap'}, dimensions={1} | all-to-all | bytes 52428800 | tf_op jit(solution)/shard_map/all_to_all | solution.py:39
  1426.1 129.2 %all-to-all-done.3 = bf16[16,640,640]{2,0,1:T(8,128)(2,1)} async-done(((bf16[16,640,640]{2,0,1:T(8,128)(2,1)}), bf16[16,640,640]{2,0,1:T(8,128)(2,1)}, u32[]{:S(2)}, u32[]{:S(2)}) %all-to-all-start.3) | async-done | bytes 13107232 | tf_op jit(solution)/shard_map/all_to_all | solution.py:42
  1620.7 39.9 fusion.284
  1660.7 69.4 fusion.394
  1730.1 90.9 fusion.64
  1820.9 293.1 %all_to_all.290 = bf16[2,128,80,640]{3,2,0,1:T(8,128)(2,1)} all-to-all(bf16[2,128,80,640]{3,2,0,1:T(8,128)(2,1)} %fusion.64), channel_id=1, replica_groups=mesh['data'=1,'dap2'=2,'dap'=4] {'dap2','dap'}, dimensions={1} | all-to-all | bytes 52428800 | tf_op jit(solution)/shard_map/all_to_all | solution.py:39
  2219.2 129.2 %all-to-all-done.5 = bf16[16,640,640]{2,0,1:T(8,128)(2,1)} async-done(((bf16[16,640,640]{2,0,1:T(8,128)(2,1)}), bf16[16,640,640]{2,0,1:T(8,128)(2,1)}, u32[]{:S(2)}, u32[]{:S(2)}) %all-to-all-start.5) | async-done | bytes 13107232 | tf_op jit(solution)/shard_map/all_to_all | solution.py:42
  2413.9 39.9 fusion.282
  2453.8 69.4 fusion.393
  2523.2 90.9 fusion.57
  2614.1 293.1 %all_to_all.291 = bf16[2,128,80,640]{3,2,0,1:T(8,128)(2,1)} all-to-all(bf16[2,128,80,640]{3,2,0,1:T(8,128)(2,1)} %fusion.57), channel_id=1, replica_groups=mesh['data'=1,'dap2'=2,'dap'=4] {'dap2','dap'}, dimensions={1} | all-to-all | bytes 52428800 | tf_op jit(solution)/shard_map/all_to_all | solution.py:39
  3007.4 129.9 %all-to-all-done.7 = bf16[16,640,640]{2,0,1:T(8,128)(2,1)} async-done(((bf16[16,640,640]{2,0,1:T(8,128)(2,1)}), bf16[16,640,640]{2,0,1:T(8,128)(2,1)}, u32[]{:S(2)}, u32[]{:S(2)}) %all-to-all-start.7) | async-done | bytes 13107232 | tf_op jit(solution)/shard_map/all_to_all | solution.py:42
  3202.6 39.9 fusion.280
  3242.6 69.4 fusion.392
  3312.0 90.9 fusion.50
  3402.9 293.1 %all_to_all.292 = bf16[2,128,80,640]{3,2,0,1:T(8,128)(2,1)} all-to-all(bf16[2,128,80,640]{3,2,0,1:T(8,128)(2,1)} %fusion.50), channel_id=1, replica_groups=mesh['data'=1,'dap2'=2,'dap'=4] {'dap2','dap'}, dimensions={1} | all-to-all | bytes 52428800 | tf_op jit(solution)/shard_map/all_to_all | solution.py:39
  3800.5 129.9 %all-to-all-done.9 = bf16[16,640,640]{2,0,1:T(8,128)(2,1)} async-done(((bf16[16,640,640]{2,0,1:T(8,128)(2,1)}), bf16[16,640,640]{2,0,1:T(8,128)(2,1)}, u32[]{:S(2)}, u32[]{:S(2)}) %all-to-all-start.9) | async-done | bytes 13107232 | tf_op jit(solution)/shard_map/all_to_all | solution.py:42
  3960.6 25.1 convert_reduce_fusion.6
  3995.8 39.9 fusion.278
  4035.8 69.4 fusion.391
  4105.2 90.9 fusion.43
  4196.0 293.1 %all_to_all.293 = bf16[2,128,80,640]{3,2,0,1:T(8,128)(2,1)} all-to-all(bf16[2,128,80,640]{3,2,0,1:T(8,128)(2,1)} %fusion.43), channel_id=1, replica_groups=mesh['data'=1,'dap2'=2,'dap'=4] {'dap2','dap'}, dimensions={1} | all-to-all | bytes 52428800 | tf_op jit(solution)/shard_map/all_to_all | solution.py:39
  4589.3 129.9 %all-to-all-done.11 = bf16[16,640,640]{2,0,1:T(8,128)(2,1)} async-done(((bf16[16,640,640]{2,0,1:T(8,128)(2,1)}), bf16[16,640,640]{2,0,1:T(8,128)(2,1)}, u32[]{:S(2)}, u32[]{:S(2)}) %all-to-all-start.11) | async-done | bytes 13107232 | tf_op jit(solution)/shard_map/all_to_all | solution.py:42
  4784.6 39.9 fusion.276
  4824.6 69.4 fusion.390
  4894.0 90.9 fusion.36
  4984.8 293.1 %all_to_all.294 = bf16[2,128,80,640]{3,2,0,1:T(8,128)(2,1)} all-to-all(bf16[2,128,80,640]{3,2,0,1:T(8,128)(2,1)} %fusion.36), channel_id=1, replica_groups=mesh['data'=1,'dap2'=2,'dap'=4] {'dap2','dap'}, dimensions={1} | all-to-all | bytes 52428800 | tf_op jit(solution)/shard_map/all_to_all | solution.py:39
  5382.4 129.9 %all-to-all-done.13 = bf16[16,640,640]{2,0,1:T(8,128)(2,1)} async-done(((bf16[16,640,640]{2,0,1:T(8,128)(2,1)}), bf16[16,640,640]{2,0,1:T(8,128)(2,1)}, u32[]{:S(2)}, u32[]{:S(2)}) %all-to-all-start.13) | async-done | bytes 13107232 | tf_op jit(solution)/shard_map/all_to_all | solution.py:42
  5542.6 25.1 convert_reduce_fusion.4
  5577.8 39.9 fusion.274
  5617.7 69.4 fusion.389
  5687.1 90.9 fusion.29
  5778.0 293.1 %all_to_all.295 = bf16[2,128,80,640]{3,2,0,1:T(8,128)(2,1)} all-to-all(bf16[2,128,80,640]{3,2,0,1:T(8,128)(2,1)} %fusion.29), channel_id=1, replica_groups=mesh['data'=1,'dap2'=2,'dap'=4] {'dap2','dap'}, dimensions={1} | all-to-all | bytes 52428800 | tf_op jit(solution)/shard_map/all_to_all | solution.py:39
  6171.3 129.9 %all-to-all-done.15 = bf16[16,640,640]{2,0,1:T(8,128)(2,1)} async-done(((bf16[16,640,640]{2,0,1:T(8,128)(2,1)}), bf16[16,640,640]{2,0,1:T(8,128)(2,1)}, u32[]{:S(2)}, u32[]{:S(2)}) %all-to-all-start.15) | async-done | bytes 13107232 | tf_op jit(solution)/shard_map/all_to_all | solution.py:42
  6366.6 39.9 fusion.272
  6406.5 69.4 fusion.388
  6475.9 90.9 fusion.22
  6566.8 293.1 %all_to_all.296 = bf16[2,128,80,640]{3,2,0,1:T(8,128)(2,1)} all-to-all(bf16[2,128,80,640]{3,2,0,1:T(8,128)(2,1)} %fusion.22), channel_id=1, replica_groups=mesh['data'=1,'dap2'=2,'dap'=4] {'dap2','dap'}, dimensions={1} | all-to-all | bytes 52428800 | tf_op jit(solution)/shard_map/all_to_all | solution.py:39
  6964.4 129.9 %all-to-all-done.17 = bf16[16,640,640]{2,0,1:T(8,128)(2,1)} async-done(((bf16[16,640,640]{2,0,1:T(8,128)(2,1)}), bf16[16,640,640]{2,0,1:T(8,128)(2,1)}, u32[]{:S(2)}, u32[]{:S(2)}) %all-to-all-start.17) | async-done | bytes 13107232 | tf_op jit(solution)/shard_map/all_to_all | solution.py:42
  7159.7 39.9 fusion.270
  7199.7 69.4 fusion.387
  7269.1 90.9 fusion.15
  7359.9 293.1 %all_to_all.297 = bf16[2,128,80,640]{3,2,0,1:T(8,128)(2,1)} all-to-all(bf16[2,128,80,640]{3,2,0,1:T(8,128)(2,1)} %fusion.15), channel_id=1, replica_groups=mesh['data'=1,'dap2'=2,'dap'=4] {'dap2','dap'}, dimensions={1} | all-to-all | bytes 52428800 | tf_op jit(solution)/shard_map/all_to_all | solution.py:39
  7753.2 129.9 %all-to-all-done.19 = bf16[16,640,640]{2,0,1:T(8,128)(2,1)} async-done(((bf16[16,640,640]{2,0,1:T(8,128)(2,1)}), bf16[16,640,640]{2,0,1:T(8,128)(2,1)}, u32[]{:S(2)}, u32[]{:S(2)}) %all-to-all-start.19) | async-done | bytes 13107232 | tf_op jit(solution)/shard_map/all_to_all | solution.py:42
  7948.5 39.9 fusion.268
  7988.4 69.4 fusion.386
  8057.8 90.9 fusion.8
  8148.7 293.1 %all_to_all.298 = bf16[2,128,80,640]{3,2,0,1:T(8,128)(2,1)} all-to-all(bf16[2,128,80,640]{3,2,0,1:T(8,128)(2,1)} %fusion.8), channel_id=1, replica_groups=mesh['data'=1,'dap2'=2,'dap'=4] {'dap2','dap'}, dimensions={1} | all-to-all | bytes 52428800 | tf_op jit(solution)/shard_map/all_to_all | solution.py:39
  8546.3 129.9 %all-to-all-done.21 = bf16[16,640,640]{2,0,1:T(8,128)(2,1)} async-done(((bf16[16,640,640]{2,0,1:T(8,128)(2,1)}), bf16[16,640,640]{2,0,1:T(8,128)(2,1)}, u32[]{:S(2)}, u32[]{:S(2)}) %all-to-all-start.21) | async-done | bytes 13107232 | tf_op jit(solution)/shard_map/all_to_all | solution.py:42
  8741.7 39.9 fusion.266
  8781.6 69.4 fusion.385
  8851.0 90.9 fusion.1
  8941.9 293.1 %all_to_all.299 = bf16[2,128,80,640]{3,2,0,1:T(8,128)(2,1)} all-to-all(bf16[2,128,80,640]{3,2,0,1:T(8,128)(2,1)} %fusion.1), channel_id=1, replica_groups=mesh['data'=1,'dap2'=2,'dap'=4] {'dap2','dap'}, dimensions={1} | all-to-all | bytes 52428800 | tf_op jit(solution)/shard_map/all_to_all | solution.py:39
  9320.6 144.3 %all-to-all-done.23 = bf16[16,640,640]{2,0,1:T(8,128)(2,1)} async-done(((bf16[16,640,640]{2,0,1:T(8,128)(2,1)}), bf16[16,640,640]{2,0,1:T(8,128)(2,1)}, u32[]{:S(2)}, u32[]{:S(2)}) %all-to-all-start.23) | async-done | bytes 13107232 | tf_op jit(solution)/shard_map/all_to_all | solution.py:42
  9522.0 27.2 fusion.167
  (501 shorter events, 1970.6 us)
Async XLA Ops:
  18.9 58.6 copy-start.104
  18.9 58.6 copy-start.106
  27.3 50.2 copy-start.16
  37.3 40.1 copy-start.40
  77.5 69.4 copy-start.60
  146.9 90.8 copy-start
  617.4 148.9 %all-to-all-start.1 = ((bf16[16,640,640]{2,0,1:T(8,128)(2,1)}), bf16[16,640,640]{2,0,1:T(8,128)(2,1)}, u32[]{:S(2)}, u32[]{:S(2)}) async-start(bf16[16,640,640]{2,0,1:T(8,128)(2,1)} %copy.572), calls=%async_computation.1 | async-start | bytes 26214400 | tf_op jit(solution)/shard_map/all_to_all | solution.py:42
  796.6 35.3 copy-start.96
  796.6 35.3 copy-start.98
  821.8 50.0 copy-start.12
  831.9 40.0 copy-start.36
  871.8 69.4 copy-start.1
  1406.4 148.9 %all-to-all-start.3 = ((bf16[16,640,640]{2,0,1:T(8,128)(2,1)}), bf16[16,640,640]{2,0,1:T(8,128)(2,1)}, u32[]{:S(2)}, u32[]{:S(2)}) async-start(bf16[16,640,640]{2,0,1:T(8,128)(2,1)} %copy.585), calls=%async_computation.3 | async-start | bytes 26214400 | tf_op jit(solution)/shard_map/all_to_all | solution.py:42
  1411.6 209.1 %copy-start.100 = (f32[128]{0:T(128)}, f32[128]{0:T(128)S(1)}, u32[]{:S(2)}) copy-start(f32[128]{0:T(128)S(1)} %get-tuple-element.94) | copy-start | bytes 1540
  1411.6 209.1 %copy-start.102 = (f32[128]{0:T(128)}, f32[128]{0:T(128)S(1)}, u32[]{:S(2)}) copy-start(f32[128]{0:T(128)S(1)} %get-tuple-element.95) | copy-start | bytes 1540
  1610.7 50.0 copy-start.14
  1620.7 40.0 copy-start.38
  1660.7 69.4 copy-start.2
  2199.5 148.9 %all-to-all-start.5 = ((bf16[16,640,640]{2,0,1:T(8,128)(2,1)}), bf16[16,640,640]{2,0,1:T(8,128)(2,1)}, u32[]{:S(2)}, u32[]{:S(2)}) async-start(bf16[16,640,640]{2,0,1:T(8,128)(2,1)} %copy.595), calls=%async_computation.5 | async-start | bytes 26214400 | tf_op jit(solution)/shard_map/all_to_all | solution.py:42
  2378.7 35.1 copy-start.94
  2403.8 50.0 copy-start.18
  2413.8 40.0 copy-start.42
  2453.8 69.4 copy-start.3
  2988.3 148.9 %all-to-all-start.7 = ((bf16[16,640,640]{2,0,1:T(8,128)(2,1)}), bf16[16,640,640]{2,0,1:T(8,128)(2,1)}, u32[]{:S(2)}, u32[]{:S(2)}) async-start(bf16[16,640,640]{2,0,1:T(8,128)(2,1)} %copy.608), calls=%async_computation.7 | async-start | bytes 26214400 | tf_op jit(solution)/shard_map/all_to_all | solution.py:42
  3192.6 50.0 copy-start.26
  3202.6 40.0 copy-start.50
  3242.6 69.4 copy-start.4
  3781.4 148.9 %all-to-all-start.9 = ((bf16[16,640,640]{2,0,1:T(8,128)(2,1)}), bf16[16,640,640]{2,0,1:T(8,128)(2,1)}, u32[]{:S(2)}, u32[]{:S(2)}) async-start(bf16[16,640,640]{2,0,1:T(8,128)(2,1)} %copy.618), calls=%async_computation.9 | async-start | bytes 26214400 | tf_op jit(solution)/shard_map/all_to_all | solution.py:42
  3960.6 35.2 copy-start.84
  3960.6 35.2 copy-start.86
  3985.8 50.0 copy-start.20
  3995.8 40.0 copy-start.44
  4035.8 69.4 copy-start.5
  4570.3 148.9 %all-to-all-start.11 = ((bf16[16,640,640]{2,0,1:T(8,128)(2,1)}), bf16[16,640,640]{2,0,1:T(8,128)(2,1)}, u32[]{:S(2)}, u32[]{:S(2)}) async-start(bf16[16,640,640]{2,0,1:T(8,128)(2,1)} %copy.631), calls=%async_computation.11 | async-start | bytes 26214400 | tf_op jit(solution)/shard_map/all_to_all | solution.py:42
  4774.5 50.0 copy-start.28
  4784.6 40.0 copy-start.52
  4824.5 69.4 copy-start.6
  5363.4 148.9 %all-to-all-start.13 = ((bf16[16,640,640]{2,0,1:T(8,128)(2,1)}), bf16[16,640,640]{2,0,1:T(8,128)(2,1)}, u32[]{:S(2)}, u32[]{:S(2)}) async-start(bf16[16,640,640]{2,0,1:T(8,128)(2,1)} %copy.641), calls=%async_computation.13 | async-start | bytes 26214400 | tf_op jit(solution)/shard_map/all_to_all | solution.py:42
  5542.6 35.2 copy-start.76
  5542.6 35.2 copy-start.78
  5567.7 50.0 copy-start.22
  5577.8 40.0 copy-start.46
  5617.7 69.4 copy-start.7
  6152.2 148.9 %all-to-all-start.15 = ((bf16[16,640,640]{2,0,1:T(8,128)(2,1)}), bf16[16,640,640]{2,0,1:T(8,128)(2,1)}, u32[]{:S(2)}, u32[]{:S(2)}) async-start(bf16[16,640,640]{2,0,1:T(8,128)(2,1)} %copy.654), calls=%async_computation.15 | async-start | bytes 26214400 | tf_op jit(solution)/shard_map/all_to_all | solution.py:42
  6356.5 50.0 copy-start.30
  6366.5 40.0 copy-start.54
  6406.5 69.4 copy-start.8
  6945.3 148.9 %all-to-all-start.17 = ((bf16[16,640,640]{2,0,1:T(8,128)(2,1)}), bf16[16,640,640]{2,0,1:T(8,128)(2,1)}, u32[]{:S(2)}, u32[]{:S(2)}) async-start(bf16[16,640,640]{2,0,1:T(8,128)(2,1)} %copy.664), calls=%async_computation.17 | async-start | bytes 26214400 | tf_op jit(solution)/shard_map/all_to_all | solution.py:42
  7124.6 35.2 copy-start.68
  7124.6 35.2 copy-start.70
  7149.7 50.0 copy-start.24
  7159.7 40.0 copy-start.48
  7199.7 69.4 copy-start.9
  7734.2 148.9 %all-to-all-start.19 = ((bf16[16,640,640]{2,0,1:T(8,128)(2,1)}), bf16[16,640,640]{2,0,1:T(8,128)(2,1)}, u32[]{:S(2)}, u32[]{:S(2)}) async-start(bf16[16,640,640]{2,0,1:T(8,128)(2,1)} %copy.677), calls=%async_computation.19 | async-start | bytes 26214400 | tf_op jit(solution)/shard_map/all_to_all | solution.py:42
  7938.4 50.0 copy-start.32
  7948.5 40.0 copy-start.56
  7988.4 69.4 copy-start.10
  8527.3 148.9 %all-to-all-start.21 = ((bf16[16,640,640]{2,0,1:T(8,128)(2,1)}), bf16[16,640,640]{2,0,1:T(8,128)(2,1)}, u32[]{:S(2)}, u32[]{:S(2)}) async-start(bf16[16,640,640]{2,0,1:T(8,128)(2,1)} %copy.687), calls=%async_computation.21 | async-start | bytes 26214400 | tf_op jit(solution)/shard_map/all_to_all | solution.py:42
  8706.5 35.2 copy-start.108
  8706.5 35.2 copy-start.110
  8731.6 50.0 copy-start.34
  8741.7 40.0 copy-start.58
  8781.6 69.4 copy-start.11
  9315.9 149.0 %all-to-all-start.23 = ((bf16[16,640,640]{2,0,1:T(8,128)(2,1)}), bf16[16,640,640]{2,0,1:T(8,128)(2,1)}, u32[]{:S(2)}, u32[]{:S(2)}) async-start(bf16[16,640,640]{2,0,1:T(8,128)(2,1)} %copy.700), calls=%async_computation.23 | async-start | bytes 26214400 | tf_op jit(solution)/shard_map/all_to_all | solution.py:42
  (81 other events, 2288.1 us)
where the time goes:
time: 9580 us; the launch traced here: 9570 us
  blocking collectives  3520 us (37%)
  local copies, waits for them, and re-layouts  1680 us (18%)
  waiting for transfers between devices  1570 us (16%)
  other arithmetic  1510 us (16%)
  matrix products  1230 us (13%)
    all_to_all x12, blocking collectives, tri_update(): ab_cols = lax.all_to_all(ab_rows, ROW_AXES, 1, 2, tiled=True)  3520 us
    all_to_all x12, waiting for transfers between devices, tri_update(): tri_rows = lax.all_to_all(tri_full, ROW_AXES, 1, 0, tiled=True)  1570 us
    convert_element_type x12, other arithmetic, row_inputs(): (mask_loc * jax.nn.sigmoid(proj_four[:, 1]) * proj_four[:, 0]).astype(jnp...  1090 us
    slice x12, local copies, waits for them, and re-layouts, row_inputs(): proj_four[:, 1]  833 us
    dot_general x12, matrix products, row_inputs(): jnp.einsum('de,ikd->eik', w_ab, x_ln, preferred_element_type=jnp.float32)  479 us
    dot_general x12, matrix products, finish_update(): jnp.einsum('cij,cd->ijd', y_ln, w_out, preferred_element_type=jnp.float32)  293 us
    convert_element_type x12, local copies, waits for them, and re-layouts, tri_update(): jnp.einsum(einsum_form, ab_cols[0], ab_cols[1], preferred_element_type=jn...  280 us
    dot_general x12, matrix products, tri_update(): jnp.einsum(einsum_form, ab_cols[0], ab_cols[1], preferred_element_type=jn...  270 us
  transfers between devices with their start and end apart: 12, of which 12 were waited for; matrix products, arithmetic and copies ran while one was open for 2% of the time, Pallas kernels for 0%

commit v1 on v0

v1 whole, which is shorter than its diff:
```python
import functools

import jax
import jax.numpy as jnp
from jax import lax
from jax.experimental import pallas as pl
from jax.experimental.pallas import tpu as pltpu
from jax.sharding import PartitionSpec as P

LN_EPS = 1e-5
ALL_ROWS = ("data", "dap2", "dap")
MESH = pl.DeviceIdType.MESH
NDEV = 8
CH = 128
SUB = CH // NDEV
RB = 16
LANES = 128
GSZ = 2
AHEAD = 3
VMEM_LIMIT = 62 * 1024 * 1024


def norm_cols(vals, gain, shift):
    mean_val = jnp.mean(vals, axis=0, keepdims=True)
    centered = vals - mean_val
    var_val = jnp.mean(centered * centered, axis=0, keepdims=True)
    return centered * lax.rsqrt(var_val + LN_EPS) * gain + shift


def sigmoid(vals):
    return 0.5 * jnp.tanh(0.5 * vals) + 0.5


def rows_kernel(do_c, do_a, ncol, *refs):
    refs = list(refs)
    z_ref = refs.pop(0)
    if do_c:
        t_ref, gip_ref, sip_ref, go_ref, so_ref, wg_ref, wo_ref = refs[:7]
        refs = refs[7:]
    if do_a:
        m_ref, gi_ref, si_ref, wab_ref = refs[:4]
        refs = refs[4:]
    if do_c:
        zo_ref = refs.pop(0)
    if do_a:
        ab_ref = refs.pop(0)
    x_ref, o_ref, g_ref = refs[:3]
    refs = refs[3:]
    if do_c:
        ts_ref, y_ref = refs[:2]
        refs = refs[2:]
    if do_a:
        p_ref, as_ref, bs_ref = refs

    if do_c:
        for c0 in range(0, CH, 16):
            for q in range(ncol // LANES):
                ts_ref[q, pl.ds(c0 * RB, 16 * RB), :] = t_ref[pl.ds(c0, 16), :, pl.ds(q * LANES, LANES)].astype(jnp.float32).reshape(16 * RB, LANES)

    def one_row(i, carry):
        chunks = [pl.ds(l0, LANES) for l0 in range(0, ncol, LANES)]
        if do_c:
            for q, ln in enumerate(chunks):
                x_ref[:, ln] = norm_cols(z_ref[i, :, ln].astype(jnp.float32), gip_ref[...], sip_ref[...]).astype(jnp.bfloat16)
                y_ref[:, ln] = norm_cols(ts_ref[q, pl.ds(i, CH, stride=RB), :], go_ref[...], so_ref[...]).astype(jnp.bfloat16)
            g_ref[...] = jnp.dot(wg_ref[...], x_ref[...], preferred_element_type=jnp.float32)
            o_ref[...] = jnp.dot(wo_ref[...], y_ref[...], preferred_element_type=jnp.float32)
            for q, ln in enumerate(chunks):
                new_z = z_ref[i, :, ln].astype(jnp.float32) + sigmoid(g_ref[:, ln]) * o_ref[:, ln]
                zo_ref[i, :, ln] = new_z.astype(jnp.bfloat16)
        src_ref = zo_ref if do_c else z_ref
        if do_a:
            for q, ln in enumerate(chunks):
                x_ref[:, ln] = norm_cols(src_ref[i, :, ln].astype(jnp.float32), gi_ref[...], si_ref[...]).astype(jnp.bfloat16)
            p_ref[...] = jnp.dot(wab_ref[...], x_ref[...], preferred_element_type=jnp.float32)
            for q, ln in enumerate(chunks):
                keep = m_ref[i, :, ln]
                as_ref[q, pl.ds(i, CH, stride=RB), :] = keep * sigmoid(p_ref[pl.ds(CH, CH), ln]) * p_ref[pl.ds(0, CH), ln]
                bs_ref[q, pl.ds(i, CH, stride=RB), :] = keep * sigmoid(p_ref[pl.ds(3 * CH, CH), ln]) * p_ref[pl.ds(2 * CH, CH), ln]
        return carry

    lax.fori_loop(0, RB, one_row, 0)
    if do_a:
        for d in range(NDEV):
            for s_ref, u in ((as_ref, 0), (bs_ref, 1)):
                for q in range(ncol // LANES):
                    ab_ref[d, :, u, :, pl.ds(q * LANES, LANES)] = s_ref[q, pl.ds(d * SUB * RB, SUB * RB), :].reshape(SUB, RB, LANES).astype(jnp.bfloat16)


def rows_call(do_c, do_a, z, t, mask, cw, aw):
    nrow, _, ncol = z.shape
    row_blk = pl.BlockSpec((RB, CH, ncol), lambda r: (r, 0, 0))

    def whole(arr):
        return pl.BlockSpec(arr.shape, lambda r: (0,) * arr.ndim)

    args, in_specs, outs, out_specs = [z], [row_blk], [], []
    scratch = [pltpu.VMEM((CH, ncol), jnp.bfloat16), pltpu.VMEM((CH, ncol), jnp.float32), pltpu.VMEM((CH, ncol), jnp.float32)]
    if do_c:
        args += [t.reshape(CH, nrow, ncol), *cw]
        in_specs += [pl.BlockSpec((CH, RB, ncol), lambda r: (0, r, 0))] + [whole(w) for w in cw]
        outs.append(jax.ShapeDtypeStruct(z.shape, jnp.bfloat16))
        out_specs.append(row_blk)
        scratch += [pltpu.VMEM((ncol // LANES, CH * RB, LANES), jnp.float32), pltpu.VMEM((CH, ncol), jnp.bfloat16)]
    if do_a:
        args += [mask, *aw]
        in_specs += [pl.BlockSpec((RB, 1, ncol), lambda r: (r, 0, 0))] + [whole(w) for w in aw]
        outs.append(jax.ShapeDtypeStruct((NDEV, SUB, 2, nrow, ncol), jnp.bfloat16))
        out_specs.append(pl.BlockSpec((NDEV, SUB, 2, RB, ncol), lambda r: (0, 0, 0, r, 0)))
        scratch += [pltpu.VMEM((4 * CH, ncol), jnp.float32), pltpu.VMEM((ncol // LANES, CH * RB, LANES), jnp.float32), pltpu.VMEM((ncol // LANES, CH * RB, LANES), jnp.float32)]
    return pl.pallas_call(
        functools.partial(rows_kernel, do_c, do_a, ncol),
        grid=(nrow // RB,),
        in_specs=in_specs,
        out_specs=out_specs,
        out_shape=outs,
        scratch_shapes=scratch,
        compiler_params=pltpu.CompilerParams(dimension_semantics=("arbitrary",), vmem_limit_bytes=VMEM_LIMIT),
        name="rows",
    )(*args)


def tri_kernel(outgoing, nrow, ncol, ab_ref, t_ref, recv, tbuf, s_ab, r_ab, s_t, r_t, l_ab, l_t):
    y_id = lax.axis_index("dap2")
    xc_id = lax.axis_index("dap")
    z_id = lax.axis_index("data")
    x_id, c_id = xc_id // 2, xc_id % 2
    me = y_id * 4 + xc_id
    ngroup = SUB // GSZ

    def peer(d):
        py, px, pc = (y_id + d // 4) % 2, (x_id + (d // 2) % 2) % 2, (c_id + d % 2) % 2
        return (z_id, py, px * 2 + pc), py * 4 + px * 2 + pc

    def chans(g):
        return pl.ds(g * GSZ, GSZ)

    def ab_copy(g, d):
        dev, num = peer(d)
        return pltpu.make_async_remote_copy(
            src_ref=ab_ref.at[num, chans(g)], dst_ref=recv.at[me, chans(g)],
            send_sem=s_ab.at[g, d], recv_sem=r_ab.at[g, d], device_id=dev, device_id_type=MESH)

    def t_copy(g, d):
        dev, num = peer(d)
        return pltpu.make_async_remote_copy(
            src_ref=tbuf.at[num, chans(g)], dst_ref=t_ref.at[me, chans(g)],
            send_sem=s_t.at[g, d], recv_sem=r_t.at[g, d], device_id=dev, device_id_type=MESH)

    def own_ab(g):
        return pltpu.make_async_copy(ab_ref.at[me, chans(g)], recv.at[me, chans(g)], l_ab.at[g])

    def own_t(g):
        return pltpu.make_async_copy(tbuf.at[me, chans(g)], t_ref.at[me, chans(g)], l_t.at[g])

    order = (6, 4, 2, 7, 5, 3, 1)

    barrier = pltpu.get_barrier_semaphore()
    for d in range(1, NDEV):
        pl.semaphore_signal(barrier, inc=1, device_id=peer(d)[0], device_id_type=MESH)
    pl.semaphore_wait(barrier, NDEV - 1)

    def send_group(g):
        for d in order:
            ab_copy(g, d).start()
        own_ab(g).start()

    for g in range(AHEAD):
        send_group(g)

    def group_step(g, carry):
        @pl.when(g < ngroup - AHEAD)
        def _():
            send_group(g + AHEAD)

        for d in order:
            ab_copy(g, d).wait_recv()
        own_ab(g).wait()
        for q in range(GSZ):
            ch = g * GSZ + q
            a_val = recv[:, ch, 0].reshape(NDEV * nrow, ncol)
            b_val = recv[:, ch, 1].reshape(NDEV * nrow, ncol)
            dims = (((1,), (1,)), ((), ())) if outgoing else (((0,), (0,)), ((), ()))
            t_val = lax.dot_general(a_val, b_val, dims, preferred_element_type=jnp.float32)
            tbuf[:, ch] = t_val.astype(jnp.bfloat16).reshape(NDEV, nrow, ncol)
        for d in order:
            t_copy(g, d).start()
        own_t(g).start()
        return carry

    lax.fori_loop(0, ngroup, group_step, 0)

    def drain(g, carry):
        for d in order:
            t_copy(g, d).wait_recv()
            t_copy(g, d).wait_send()
            ab_copy(g, d).wait_send()
        own_t(g).wait()
        return carry

    lax.fori_loop(0, ngroup, drain, 0)


def tri_call(outgoing, ab):
    _, _, _, nrow, ncol = ab.shape
    ngroup = SUB // GSZ
    sems = pltpu.SemaphoreType.DMA((ngroup, NDEV))
    return pl.pallas_call(
        functools.partial(tri_kernel, outgoing, nrow, ncol),
        in_specs=[pl.BlockSpec(memory_space=pl.ANY)],
        out_specs=pl.BlockSpec(memory_space=pl.ANY),
        out_shape=jax.ShapeDtypeStruct((NDEV, SUB, nrow, ncol), jnp.bfloat16),
        scratch_shapes=[
            pltpu.VMEM((NDEV, SUB, 2, nrow, ncol), jnp.bfloat16),
            pltpu.VMEM((NDEV, SUB, nrow, ncol), jnp.bfloat16),
            sems, sems, sems, sems,
            pltpu.SemaphoreType.DMA((ngroup,)), pltpu.SemaphoreType.DMA((ngroup,)),
        ],
        compiler_params=pltpu.CompilerParams(collective_id=0 if outgoing else 1, has_side_effects=True, vmem_limit_bytes=VMEM_LIMIT),
        name="tri_out" if outgoing else "tri_in",
    )(ab)


def solution(mesh):
    row_spec = P(ALL_ROWS, None, None)
    mask_spec = P(ALL_ROWS, None)

    def local_stack(pair_rep, pair_mask, norm_in, norm_out, w_ab, w_gate, w_out):
        mask_f = pair_mask.astype(jnp.float32)[:, None, :]
        norm_in = norm_in.astype(jnp.float32)[..., None]
        norm_out = norm_out.astype(jnp.float32)[..., None]
        w_ab = jnp.swapaxes(w_ab, -1, -2)
        w_gate = jnp.swapaxes(w_gate, -1, -2)
        w_out = jnp.swapaxes(w_out, -1, -2)
        n_layers = w_ab.shape[0]

        def cw(l, u):
            return (norm_in[l, u, 0], norm_in[l, u, 1], norm_out[l, u, 0], norm_out[l, u, 1], w_gate[l, u], w_out[l, u])

        def aw(l, u):
            return (norm_in[l, u, 0], norm_in[l, u, 1], w_ab[l, u])

        def layer(l, z, ab):
            t = tri_call(True, ab)
            z, ab = rows_call(True, True, z, t, mask_f, cw(l, 0), aw(l, 1))
            return z, tri_call(False, ab)

        def body(l, state):
            z, t = layer(l, *state)
            return tuple(rows_call(True, True, z, t, mask_f, cw(l, 1), aw(l + 1, 0)))

        z = jnp.swapaxes(pair_rep, 1, 2)
        ab, = rows_call(False, True, z, None, mask_f, None, aw(0, 0))
        z, ab = lax.fori_loop(0, n_layers - 1, body, (z, ab))
        z, t = layer(n_layers - 1, z, ab)
        z, = rows_call(True, False, z, t, mask_f, cw(n_layers - 1, 1), None)
        return jnp.swapaxes(z, 1, 2)

    return jax.shard_map(local_stack, mesh=mesh, in_specs=(row_spec, mask_spec, P(), P(), P(), P(), P()), out_specs=row_spec, check_vma=False)
```

time: 9580 us -> 6620 us (0.69)
  Pallas kernels: 0 us -> 6520 us
  blocking collectives: 3520 us -> 0 us
  local copies, waits for them, and re-layouts: 1680 us -> 98.5 us
  waiting for transfers between devices: 1570 us -> 0 us
  other arithmetic: 1510 us -> 1.65 us
  matrix products: 1230 us -> 0 us
    pallas_call x0 -> x25, Pallas kernels: none -> 6520 us  [the longest x12 5130 us: tri_call(): pl.pallas_call(functools.partial(tri_kernel, outgoing, nrow, ncol), in_sp...]
    all_to_all x12 -> x0, blocking collectives: 3520 us -> none  [tri_update(): ab_cols = lax.all_to_all(ab_rows, ROW_AXES, 1, 2, tiled=True)]
    all_to_all x12 -> x0, waiting for transfers between devices: 1570 us -> none  [tri_update(): tri_rows = lax.all_to_all(tri_full, ROW_AXES, 1, 0, tiled=True)]
    dot_general x48 -> x0, matrix products: 1230 us -> none  [the longest x12 479 us: row_inputs(): jnp.einsum('de,ikd->eik', w_ab, x_ln, preferred_element_type=jnp.float32)]
    convert_element_type x29 -> x1, other arithmetic: 1200 us -> 0.94 us  [local_stack(): mask_f = pair_mask.astype(jnp.float32)[:, None, :]]
    slice x36 -> x0, local copies, waits for them, and re-layouts: 1060 us -> none  [the longest x12 833 us: row_inputs(): proj_four[:, 1]]
    convert_element_type x51 -> x0, local copies, waits for them, and re-layouts: 371 us -> none  [the longest x12 280 us: tri_update(): jnp.einsum(einsum_form, ab_cols[0], ab_cols[1], preferred_element_type=jn...]
    reduce_sum x37 -> x0, other arithmetic: 311 us -> none  [the longest x24 222 us: layer_norm(): var_val = jnp.mean(centered * centered, axis=norm_axis, keepdims=True)]
  transfers between devices with their start and end apart: 12 -> 0, of which waited for: 12 -> 0; matrix products, arithmetic and copies ran while one was open for 2% -> 0% of each run, Pallas kernels for 0% -> 0%
where the time goes in v1:
time: 6620 us
  Pallas kernels  6520 us (98%)
  local copies, waits for them, and re-layouts  98.5 us (1%)
    pallas_call x12, Pallas kernels, tri_call(): pl.pallas_call(functools.partial(tri_kernel, outgoing, nrow, ncol), in_sp...  5130 us
    pallas_call x13, Pallas kernels, rows_call(): pl.pallas_call(functools.partial(rows_kernel, do_c, do_a, ncol), grid=(nr...  1390 us

profile of v1, /device:TPU:0, one launch (start us, length us, event | category | flops | bytes accessed | tf_op | source)
XLA Modules:
  0.0 6623.3 jit_solution(17647078916920938270)
XLA Ops:
  1.3 0.7 copy.22.refs_2_
  2.8 1.9 copy.21
  5.4 0.9 convert_element_type.2
  6.5 17.5 copy.20
  24.0 67.8 %rows.19 = bf16[8,16,2,80,640]{4,3,2,1,0:T(8,128)(2,1)} custom-call(bf16[80,128,640]{2,1,0:T(8,128)(2,1)} %bitcast.87, f32[80,1,640]{2,1,0:T(1,128)S(1)} %broadcast_in_dim.15.refs_1_.refs_8_, f32[128,1]{1,0:T(8,128)} %copy.22.refs_2_, f32[128,1]{1,0:T(8,128)} %copy.23.refs_3_, bf16[512,128]{1,0:T(8,128)(2,1)} %get-tuple-element.281.refs_4_), custom_call_target="tpu_custom_call" | custom-call | tf_op jit(solution)/shard_map/rows/pallas_call | solution.py:111
  91.8 1.9 copy.24
  93.7 1.9 copy.25
  95.6 5474.5 %while.17 = (s32[]{:T(128)}, bf16[80,128,640]{2,1,0:T(8,128)(2,1)}, bf16[8,16,2,80,640]{4,3,2,1,0:T(8,128)(2,1)}, f32[6,2,2,128,1]{3,4,2,1,0:T(1,128)S(1)}, f32[...) while((s32[]{:T(128)}, bf16[80,128,640]{2,1,0:T(8,128)(2,1)}, ...), condition=%wide.region_1.0_spmd, body=%wide.region_0.0_spmd.sunk | while | flops 5 | bytes 807091 | solution.py:254
  98.6 0.7 copy.49.refs_4_
  99.4 0.7 copy.50.refs_5_
  100.1 0.7 dynamic-slice_bitcast_fusion.9
  100.8 1.5 dynamic-slice_bitcast_fusion.8
  102.3 429.5 %tri_out.10 = bf16[8,16,80,640]{3,2,1,0:T(8,128)(2,1)} custom-call(bf16[8,16,2,80,640]{4,3,2,1,0:T(8,128)(2,1)} %get-tuple-element.407.ab_ref), custom_call_target="tpu_custom_call" | custom-call | tf_op jit(solution)/shard_map/while/body/eval_jaxpr/tri_out/pallas_call | solution.py:208
  531.8 115.2 %rows.22 = (bf16[80,128,640]{2,1,0:T(8,128)(2,1)}, bf16[8,16,2,80,640]{4,3,2,1,0:T(8,128)(2,1)}) custom-call(bf16[80,128,640]{2,1,0:T(8,128)(2,1)} %get-tuple-element.406.refs_0_, bf16[128,80,640]{2,1,0:T(8,128)(2,1)} %bitcast.86, f32[128,1]{1,0:T(8,128)} %copy.47.refs_2_, f32[128,1]{1,0:T(8,128)} %copy.48.refs_3_, f32[128,1]{1,0:T(8,128)} %copy.49.refs_4_, ...), custom_call_target="tpu_custom_call" | custom-call | tf_op jit(solution)/shard_map/while/body/eval_jaxpr/rows/pallas_call | solution.py:111
  647.0 427.3 %tri_in.10 = bf16[8,16,80,640]{3,2,1,0:T(8,128)(2,1)} custom-call(bf16[8,16,2,80,640]{4,3,2,1,0:T(8,128)(2,1)} %get-tuple-element.383.ab_ref), custom_call_target="tpu_custom_call" | custom-call | tf_op jit(solution)/shard_map/while/body/eval_jaxpr/tri_in/pallas_call | solution.py:208
  1074.4 0.7 copy.53.refs_4_
  1077.3 115.2 %rows.23 = (bf16[80,128,640]{2,1,0:T(8,128)(2,1)}, bf16[8,16,2,80,640]{4,3,2,1,0:T(8,128)(2,1)}) custom-call(bf16[80,128,640]{2,1,0:T(8,128)(2,1)} %get-tuple-element.382.refs_0_, bf16[128,80,640]{2,1,0:T(8,128)(2,1)} %bitcast.85, f32[128,1]{1,0:T(8,128)} %copy.51.refs_9_.refs_2_, f32[128,1]{1,0:T(8,128)} %copy.52.refs_10_.refs_3_, f32[128,1]{1,0:T(8,128)} %copy.53.refs_4_, ...), custom_call_target="tpu_custom_call" | custom-call | tf_op jit(solution)/shard_map/while/body/eval_jaxpr/rows/pallas_call | solution.py:111
  1195.4 0.7 copy.49.refs_4_
  1196.1 0.7 copy.50.refs_5_
  1196.8 0.7 dynamic-slice_bitcast_fusion.9
  1197.6 1.5 dynamic-slice_bitcast_fusion.8
  1199.0 427.2 %tri_out.10 = bf16[8,16,80,640]{3,2,1,0:T(8,128)(2,1)} custom-call(bf16[8,16,2,80,640]{4,3,2,1,0:T(8,128)(2,1)} %get-tuple-element.407.ab_ref), custom_call_target="tpu_custom_call" | custom-call | tf_op jit(solution)/shard_map/while/body/eval_jaxpr/tri_out/pallas_call | solution.py:208
  1626.3 115.2 %rows.22 = (bf16[80,128,640]{2,1,0:T(8,128)(2,1)}, bf16[8,16,2,80,640]{4,3,2,1,0:T(8,128)(2,1)}) custom-call(bf16[80,128,640]{2,1,0:T(8,128)(2,1)} %get-tuple-element.406.refs_0_, bf16[128,80,640]{2,1,0:T(8,128)(2,1)} %bitcast.86, f32[128,1]{1,0:T(8,128)} %copy.47.refs_2_, f32[128,1]{1,0:T(8,128)} %copy.48.refs_3_, f32[128,1]{1,0:T(8,128)} %copy.49.refs_4_, ...), custom_call_target="tpu_custom_call" | custom-call | tf_op jit(solution)/shard_map/while/body/eval_jaxpr/rows/pallas_call | solution.py:111
  1741.5 427.3 %tri_in.10 = bf16[8,16,80,640]{3,2,1,0:T(8,128)(2,1)} custom-call(bf16[8,16,2,80,640]{4,3,2,1,0:T(8,128)(2,1)} %get-tuple-element.383.ab_ref), custom_call_target="tpu_custom_call" | custom-call | tf_op jit(solution)/shard_map/while/body/eval_jaxpr/tri_in/pallas_call | solution.py:208
  2168.8 0.7 copy.53.refs_4_
  2171.7 115.2 %rows.23 = (bf16[80,128,640]{2,1,0:T(8,128)(2,1)}, bf16[8,16,2,80,640]{4,3,2,1,0:T(8,128)(2,1)}) custom-call(bf16[80,128,640]{2,1,0:T(8,128)(2,1)} %get-tuple-element.382.refs_0_, bf16[128,80,640]{2,1,0:T(8,128)(2,1)} %bitcast.85, f32[128,1]{1,0:T(8,128)} %copy.51.refs_9_.refs_2_, f32[128,1]{1,0:T(8,128)} %copy.52.refs_10_.refs_3_, f32[128,1]{1,0:T(8,128)} %copy.53.refs_4_, ...), custom_call_target="tpu_custom_call" | custom-call | tf_op jit(solution)/shard_map/while/body/eval_jaxpr/rows/pallas_call | solution.py:111
  2289.8 0.7 copy.49.refs_4_
  2290.6 0.7 copy.50.refs_5_
  2291.3 0.7 dynamic-slice_bitcast_fusion.9
  2292.0 1.5 dynamic-slice_bitcast_fusion.8
  2293.5 427.2 %tri_out.10 = bf16[8,16,80,640]{3,2,1,0:T(8,128)(2,1)} custom-call(bf16[8,16,2,80,640]{4,3,2,1,0:T(8,128)(2,1)} %get-tuple-element.407.ab_ref), custom_call_target="tpu_custom_call" | custom-call | tf_op jit(solution)/shard_map/while/body/eval_jaxpr/tri_out/pallas_call | solution.py:208
  2720.7 115.2 %rows.22 = (bf16[80,128,640]{2,1,0:T(8,128)(2,1)}, bf16[8,16,2,80,640]{4,3,2,1,0:T(8,128)(2,1)}) custom-call(bf16[80,128,640]{2,1,0:T(8,128)(2,1)} %get-tuple-element.406.refs_0_, bf16[128,80,640]{2,1,0:T(8,128)(2,1)} %bitcast.86, f32[128,1]{1,0:T(8,128)} %copy.47.refs_2_, f32[128,1]{1,0:T(8,128)} %copy.48.refs_3_, f32[128,1]{1,0:T(8,128)} %copy.49.refs_4_, ...), custom_call_target="tpu_custom_call" | custom-call | tf_op jit(solution)/shard_map/while/body/eval_jaxpr/rows/pallas_call | solution.py:111
  2835.9 427.3 %tri_in.10 = bf16[8,16,80,640]{3,2,1,0:T(8,128)(2,1)} custom-call(bf16[8,16,2,80,640]{4,3,2,1,0:T(8,128)(2,1)} %get-tuple-element.383.ab_ref), custom_call_target="tpu_custom_call" | custom-call | tf_op jit(solution)/shard_map/while/body/eval_jaxpr/tri_in/pallas_call | solution.py:208
  3263.2 0.7 copy.53.refs_4_
  3266.1 115.2 %rows.23 = (bf16[80,128,640]{2,1,0:T(8,128)(2,1)}, bf16[8,16,2,80,640]{4,3,2,1,0:T(8,128)(2,1)}) custom-call(bf16[80,128,640]{2,1,0:T(8,128)(2,1)} %get-tuple-element.382.refs_0_, bf16[128,80,640]{2,1,0:T(8,128)(2,1)} %bitcast.85, f32[128,1]{1,0:T(8,128)} %copy.51.refs_9_.refs_2_, f32[128,1]{1,0:T(8,128)} %copy.52.refs_10_.refs_3_, f32[128,1]{1,0:T(8,128)} %copy.53.refs_4_, ...), custom_call_target="tpu_custom_call" | custom-call | tf_op jit(solution)/shard_map/while/body/eval_jaxpr/rows/pallas_call | solution.py:111
  3384.3 0.7 copy.49.refs_4_
  3385.0 0.7 copy.50.refs_5_
  3385.7 0.7 dynamic-slice_bitcast_fusion.9
  3386.5 1.5 dynamic-slice_bitcast_fusion.8
  3387.9 427.2 %tri_out.10 = bf16[8,16,80,640]{3,2,1,0:T(8,128)(2,1)} custom-call(bf16[8,16,2,80,640]{4,3,2,1,0:T(8,128)(2,1)} %get-tuple-element.407.ab_ref), custom_call_target="tpu_custom_call" | custom-call | tf_op jit(solution)/shard_map/while/body/eval_jaxpr/tri_out/pallas_call | solution.py:208
  3815.1 115.2 %rows.22 = (bf16[80,128,640]{2,1,0:T(8,128)(2,1)}, bf16[8,16,2,80,640]{4,3,2,1,0:T(8,128)(2,1)}) custom-call(bf16[80,128,640]{2,1,0:T(8,128)(2,1)} %get-tuple-element.406.refs_0_, bf16[128,80,640]{2,1,0:T(8,128)(2,1)} %bitcast.86, f32[128,1]{1,0:T(8,128)} %copy.47.refs_2_, f32[128,1]{1,0:T(8,128)} %copy.48.refs_3_, f32[128,1]{1,0:T(8,128)} %copy.49.refs_4_, ...), custom_call_target="tpu_custom_call" | custom-call | tf_op jit(solution)/shard_map/while/body/eval_jaxpr/rows/pallas_call | solution.py:111
  3930.3 427.3 %tri_in.10 = bf16[8,16,80,640]{3,2,1,0:T(8,128)(2,1)} custom-call(bf16[8,16,2,80,640]{4,3,2,1,0:T(8,128)(2,1)} %get-tuple-element.383.ab_ref), custom_call_target="tpu_custom_call" | custom-call | tf_op jit(solution)/shard_map/while/body/eval_jaxpr/tri_in/pallas_call | solution.py:208
  4357.7 0.7 copy.53.refs_4_
  4360.6 115.2 %rows.23 = (bf16[80,128,640]{2,1,0:T(8,128)(2,1)}, bf16[8,16,2,80,640]{4,3,2,1,0:T(8,128)(2,1)}) custom-call(bf16[80,128,640]{2,1,0:T(8,128)(2,1)} %get-tuple-element.382.refs_0_, bf16[128,80,640]{2,1,0:T(8,128)(2,1)} %bitcast.85, f32[128,1]{1,0:T(8,128)} %copy.51.refs_9_.refs_2_, f32[128,1]{1,0:T(8,128)} %copy.52.refs_10_.refs_3_, f32[128,1]{1,0:T(8,128)} %copy.53.refs_4_, ...), custom_call_target="tpu_custom_call" | custom-call | tf_op jit(solution)/shard_map/while/body/eval_jaxpr/rows/pallas_call | solution.py:111
  4478.7 0.7 copy.49.refs_4_
  4479.4 0.7 copy.50.refs_5_
  4480.2 0.7 dynamic-slice_bitcast_fusion.9
  4480.9 1.5 dynamic-slice_bitcast_fusion.8
  4482.4 427.2 %tri_out.10 = bf16[8,16,80,640]{3,2,1,0:T(8,128)(2,1)} custom-call(bf16[8,16,2,80,640]{4,3,2,1,0:T(8,128)(2,1)} %get-tuple-element.407.ab_ref), custom_call_target="tpu_custom_call" | custom-call | tf_op jit(solution)/shard_map/while/body/eval_jaxpr/tri_out/pallas_call | solution.py:208
  4909.6 115.2 %rows.22 = (bf16[80,128,640]{2,1,0:T(8,128)(2,1)}, bf16[8,16,2,80,640]{4,3,2,1,0:T(8,128)(2,1)}) custom-call(bf16[80,128,640]{2,1,0:T(8,128)(2,1)} %get-tuple-element.406.refs_0_, bf16[128,80,640]{2,1,0:T(8,128)(2,1)} %bitcast.86, f32[128,1]{1,0:T(8,128)} %copy.47.refs_2_, f32[128,1]{1,0:T(8,128)} %copy.48.refs_3_, f32[128,1]{1,0:T(8,128)} %copy.49.refs_4_, ...), custom_call_target="tpu_custom_call" | custom-call | tf_op jit(solution)/shard_map/while/body/eval_jaxpr/rows/pallas_call | solution.py:111
  5024.8 427.3 %tri_in.10 = bf16[8,16,80,640]{3,2,1,0:T(8,128)(2,1)} custom-call(bf16[8,16,2,80,640]{4,3,2,1,0:T(8,128)(2,1)} %get-tuple-element.383.ab_ref), custom_call_target="tpu_custom_call" | custom-call | tf_op jit(solution)/shard_map/while/body/eval_jaxpr/tri_in/pallas_call | solution.py:208
  5452.1 0.7 copy.53.refs_4_
  5455.0 115.2 %rows.23 = (bf16[80,128,640]{2,1,0:T(8,128)(2,1)}, bf16[8,16,2,80,640]{4,3,2,1,0:T(8,128)(2,1)}) custom-call(bf16[80,128,640]{2,1,0:T(8,128)(2,1)} %get-tuple-element.382.refs_0_, bf16[128,80,640]{2,1,0:T(8,128)(2,1)} %bitcast.85, f32[128,1]{1,0:T(8,128)} %copy.51.refs_9_.refs_2_, f32[128,1]{1,0:T(8,128)} %copy.52.refs_10_.refs_3_, f32[128,1]{1,0:T(8,128)} %copy.53.refs_4_, ...), custom_call_target="tpu_custom_call" | custom-call | tf_op jit(solution)/shard_map/while/body/eval_jaxpr/rows/pallas_call | solution.py:111
  5570.2 427.2 %tri_out.9 = bf16[8,16,80,640]{3,2,1,0:T(8,128)(2,1)} custom-call(bf16[8,16,2,80,640]{4,3,2,1,0:T(8,128)(2,1)} %get-tuple-element.235.ab_ref), custom_call_target="tpu_custom_call" | custom-call | tf_op jit(solution)/shard_map/tri_out/pallas_call | solution.py:208
  5997.5 0.7 copy.30.refs_9_.refs_2_
  5998.2 0.7 copy.31.refs_10_.refs_3_
  5999.0 0.7 copy.26.refs_2_
  6000.4 1.5 slice_bitcast_fusion.2
  6001.9 0.7 copy.28.refs_4_
  6003.3 115.2 %rows.20 = (bf16[80,128,640]{2,1,0:T(8,128)(2,1)}, bf16[8,16,2,80,640]{4,3,2,1,0:T(8,128)(2,1)}) custom-call(bf16[80,128,640]{2,1,0:T(8,128)(2,1)} %get-tuple-element.234.refs_0_, bf16[128,80,640]{2,1,0:T(8,128)(2,1)} %bitcast.89, f32[128,1]{1,0:T(8,128)} %copy.26.refs_2_, f32[128,1]{1,0:T(8,128)} %copy.27.refs_3_, f32[128,1]{1,0:T(8,128)} %copy.28.refs_4_, ...), custom_call_target="tpu_custom_call" | custom-call | tf_op jit(solution)/shard_map/rows/pallas_call | solution.py:111
  6118.5 427.3 %tri_in.9 = bf16[8,16,80,640]{3,2,1,0:T(8,128)(2,1)} custom-call(bf16[8,16,2,80,640]{4,3,2,1,0:T(8,128)(2,1)} %get-tuple-element.237.ab_ref), custom_call_target="tpu_custom_call" | custom-call | tf_op jit(solution)/shard_map/tri_in/pallas_call | solution.py:208
  6545.8 0.7 copy.34.refs_4_
  6547.3 58.5 rows.21
  6605.8 17.5 copy.36
  (60 shorter events, 30.6 us)
Async XLA Ops:
  24.0 71.6 %copy-start = (bf16[6,2,2,128]{3,2,1,0:T(2,128)(2,1)S(1)}, bf16[6,2,2,128]{3,2,1,0:T(2,128)(2,1)}, u32[]{:S(2)}) copy-start(bf16[6,2,2,128]{3,2,1,0:T(2,128)(2,1)} %param.12) | copy-start | bytes 18436
  5570.2 427.3 %copy-start.4 = (f32[128,1]{0,1:T(1,128)S(1)}, f32[128,1]{0,1:T(1,128)}, u32[]{:S(2)}) copy-start(f32[128,1]{0,1:T(1,128)} %get-tuple-element.291) | copy-start | bytes 1540
  5570.2 428.0 %copy-start.3 = (f32[128,1]{0,1:T(1,128)S(1)}, f32[128,1]{0,1:T(1,128)}, u32[]{:S(2)}) copy-start(f32[128,1]{0,1:T(1,128)} %get-tuple-element.290) | copy-start | bytes 1540
  5570.2 428.8 %copy-start.2 = (f32[128,1]{0,1:T(1,128)S(1)}, f32[128,1]{0,1:T(1,128)}, u32[]{:S(2)}) copy-start(f32[128,1]{0,1:T(1,128)} %get-tuple-element.293) | copy-start | bytes 1540
  5570.2 429.5 %copy-start.1 = (f32[128,1]{0,1:T(1,128)S(1)}, f32[128,1]{0,1:T(1,128)}, u32[]{:S(2)}) copy-start(f32[128,1]{0,1:T(1,128)} %get-tuple-element.292) | copy-start | bytes 1540

commit v2 on v0

v2 whole, which is shorter than its diff:
```python
import functools

import jax
import jax.numpy as jnp
from jax import lax
from jax.experimental import pallas as pl
from jax.experimental.pallas import tpu as pltpu
from jax.sharding import PartitionSpec as P

LN_EPS = 1e-5
ALL_ROWS = ("data", "dap2", "dap")
MESH = pl.DeviceIdType.MESH
NDEV = 8
CH = 128
SUB = CH // NDEV
RB = 16
LANES = 128
VMEM_LIMIT = 62 * 1024 * 1024
ORDER = (6, 4, 2, 7, 5, 3, 1)


def norm_cols(vals, gain, shift):
    mean_val = jnp.mean(vals, axis=0, keepdims=True)
    centered = vals - mean_val
    var_val = jnp.mean(centered * centered, axis=0, keepdims=True)
    return centered * lax.rsqrt(var_val + LN_EPS) * gain + shift


def sigmoid(vals):
    return 0.5 * jnp.tanh(0.5 * vals) + 0.5


def update_kernel(do_c, do_a, outgoing, nrow, ncol, *refs):
    refs = list(refs)

    def take(count):
        out = refs[:count]
        del refs[:count]
        return out

    z_ref, = take(1)
    if do_c:
        t_ref, gip_ref, sip_ref, go_ref, so_ref, wg_ref, wo_ref = take(7)
    if do_a:
        m_ref, gi_ref, si_ref, wab_ref = take(4)
    if do_c:
        zo_ref, tr_ref = take(2)
    if do_a:
        tn_ref, ab_ref = take(2)
    zbuf, scr, x_ref, l_z = take(4)
    if do_c:
        o_ref, g_ref, y_ref, tblk, s_t, r_t, l_t = take(7)
    if do_a:
        p_ref, scr_b, abblk, recv, tst, s_ab, r_ab, l_ab, l_st, l_tn = take(10)

    y_id = lax.axis_index("dap2")
    xc_id = lax.axis_index("dap")
    z_id = lax.axis_index("data")
    x_id, c_id = xc_id // 2, xc_id % 2
    me = y_id * 4 + xc_id
    nblk = nrow // RB
    nlane = ncol // LANES

    def peer(d):
        py, px, pc = (y_id + d // 4) % 2, (x_id + (d // 2) % 2) % 2, (c_id + d % 2) % 2
        return (z_id, py, px * 2 + pc), py * 4 + px * 2 + pc

    def rows(r):
        return pl.ds(r * RB, RB)

    def t_copy(r, d):
        dev, num = peer(d)
        return pltpu.make_async_remote_copy(
            src_ref=t_ref.at[num, :, rows(r)], dst_ref=tr_ref.at[me, :, rows(r)],
            send_sem=s_t.at[r, d], recv_sem=r_t.at[r, d], device_id=dev, device_id_type=MESH)

    def ab_copy(r, d):
        dev, num = peer(d)
        return pltpu.make_async_remote_copy(
            src_ref=ab_ref.at[num, :, :, rows(r)], dst_ref=recv.at[me, :, :, rows(r)],
            send_sem=s_ab.at[r, d], recv_sem=r_ab.at[r, d], device_id=dev, device_id_type=MESH)

    def own_ab(r):
        return pltpu.make_async_copy(ab_ref.at[me, :, :, rows(r)], recv.at[me, :, :, rows(r)], l_ab.at[r])

    def stage_ab(r):
        return pltpu.make_async_copy(abblk, ab_ref.at[:, :, :, rows(r)], l_st)

    def load_t(r, d):
        num = peer(d)[1]
        src_ref = t_ref if d == 0 else tr_ref
        return pltpu.make_async_copy(src_ref.at[num, :, rows(r)], tblk.at[num], l_t.at[d])

    def load_z(r):
        return pltpu.make_async_copy(z_ref.at[rows(r)], zbuf, l_z)

    def store_z(r):
        return pltpu.make_async_copy(zbuf, zo_ref.at[rows(r)], l_z)

    barrier = pltpu.get_barrier_semaphore()
    for d in range(1, NDEV):
        pl.semaphore_signal(barrier, inc=1, device_id=peer(d)[0], device_id_type=MESH)
    pl.semaphore_wait(barrier, NDEV - 1)

    if do_c:
        for r in range(nblk):
            for d in ORDER:
                t_copy(r, d).start()

    chunks = [pl.ds(l0, LANES) for l0 in range(0, ncol, LANES)]

    def one_row(r, i):
        if do_c:
            for q, ln in enumerate(chunks):
                x_ref[:, ln] = norm_cols(zbuf[i, :, ln].astype(jnp.float32), gip_ref[...], sip_ref[...]).astype(jnp.bfloat16)
                y_ref[:, ln] = norm_cols(scr[q, pl.ds(i, CH, stride=RB), :], go_ref[...], so_ref[...]).astype(jnp.bfloat16)
            g_ref[...] = jnp.dot(wg_ref[...], x_ref[...], preferred_element_type=jnp.float32)
            o_ref[...] = jnp.dot(wo_ref[...], y_ref[...], preferred_element_type=jnp.float32)
            for q, ln in enumerate(chunks):
                new_z = zbuf[i, :, ln].astype(jnp.float32) + sigmoid(g_ref[:, ln]) * o_ref[:, ln]
                zbuf[i, :, ln] = new_z.astype(jnp.bfloat16)
        if do_a:
            for q, ln in enumerate(chunks):
                x_ref[:, ln] = norm_cols(zbuf[i, :, ln].astype(jnp.float32), gi_ref[...], si_ref[...]).astype(jnp.bfloat16)
            p_ref[...] = jnp.dot(wab_ref[...], x_ref[...], preferred_element_type=jnp.float32)
            for q, ln in enumerate(chunks):
                keep = m_ref[r * RB + i, :, ln]
                scr[q, pl.ds(i, CH, stride=RB), :] = keep * sigmoid(p_ref[pl.ds(CH, CH), ln]) * p_ref[pl.ds(0, CH), ln]
                scr_b[q, pl.ds(i, CH, stride=RB), :] = keep * sigmoid(p_ref[pl.ds(3 * CH, CH), ln]) * p_ref[pl.ds(2 * CH, CH), ln]

    def block_step(r, carry):
        load_z(r).start()
        if do_c:
            for d in ORDER:
                t_copy(r, d).wait_recv()
            for d in range(NDEV):
                load_t(r, d).start()
            for d in range(NDEV):
                load_t(r, d).wait()
            for s in range(NDEV):
                for q, ln in enumerate(chunks):
                    scr[q, pl.ds(s * SUB * RB, SUB * RB), :] = tblk[s, :, :, ln].astype(jnp.float32).reshape(SUB * RB, LANES)
        load_z(r).wait()

        def row_step(i, inner):
            one_row(r, i)
            return inner

        lax.fori_loop(0, RB, row_step, 0)
        if do_c:
            store_z(r).start()
        if do_a:
            for d in range(NDEV):
                for s_ref, u in ((scr, 0), (scr_b, 1)):
                    for q, ln in enumerate(chunks):
                        abblk[d, :, u, :, ln] = s_ref[q, pl.ds(d * SUB * RB, SUB * RB), :].reshape(SUB, RB, LANES).astype(jnp.bfloat16)
            stage_ab(r).start()
            stage_ab(r).wait()
            for d in ORDER:
                ab_copy(r, d).start()
            own_ab(r).start()
        if do_c:
            store_z(r).wait()
        return carry

    lax.fori_loop(0, nblk, block_step, 0)

    if do_a:
        def wait_ab(r, carry):
            for d in ORDER:
                ab_copy(r, d).wait_recv()
            own_ab(r).wait()
            return carry

        lax.fori_loop(0, nblk, wait_ab, 0)

        def put_t(ch):
            return pltpu.make_async_copy(tst.at[ch % 2], tn_ref.at[:, ch], l_tn.at[ch % 2])

        def chan_step(ch, carry):
            a_val = recv[:, ch, 0].reshape(NDEV * nrow, ncol)
            b_val = recv[:, ch, 1].reshape(NDEV * nrow, ncol)
            dims = (((1,), (1,)), ((), ())) if outgoing else (((0,), (0,)), ((), ()))
            t_val = lax.dot_general(a_val, b_val, dims, preferred_element_type=jnp.float32)

            @pl.when(ch >= 2)
            def _():
                put_t(ch - 2).wait()

            tst[ch % 2] = t_val.astype(jnp.bfloat16).reshape(NDEV, nrow, ncol)
            put_t(ch).start()
            return carry

        lax.fori_loop(0, SUB, chan_step, 0)
        put_t(SUB - 2).wait()
        put_t(SUB - 1).wait()

    def drain(r, carry):
        for d in ORDER:
            if do_c:
                t_copy(r, d).wait_send()
            if do_a:
                ab_copy(r, d).wait_send()
        return carry

    lax.fori_loop(0, nblk, drain, 0)


def update_call(do_c, do_a, outgoing, cid, z, t, mask, cw, aw):
    nrow, _, ncol = z.shape
    nblk = nrow // RB
    hbm = pl.BlockSpec(memory_space=pl.ANY)
    vmem = pl.BlockSpec(memory_space=pltpu.VMEM)
    sems = pltpu.SemaphoreType.DMA((nblk, NDEV))
    strided = pltpu.VMEM((ncol // LANES, CH * RB, LANES), jnp.float32)
    t_shape = jax.ShapeDtypeStruct((NDEV, SUB, nrow, ncol), jnp.bfloat16)
    args, in_specs, outs = [z], [hbm], []
    scratch = [pltpu.VMEM((RB, CH, ncol), jnp.bfloat16), strided, pltpu.VMEM((CH, ncol), jnp.bfloat16), pltpu.SemaphoreType.DMA]
    if do_c:
        args += [t, *cw]
        in_specs += [hbm] + [vmem] * len(cw)
        outs += [jax.ShapeDtypeStruct(z.shape, jnp.bfloat16), t_shape]
        scratch += [pltpu.VMEM((CH, ncol), jnp.float32), pltpu.VMEM((CH, ncol), jnp.float32), pltpu.VMEM((CH, ncol), jnp.bfloat16),
                    pltpu.VMEM((NDEV, SUB, RB, ncol), jnp.bfloat16), sems, sems, pltpu.SemaphoreType.DMA((NDEV,))]
    if do_a:
        args += [mask, *aw]
        in_specs += [vmem] * (1 + len(aw))
        outs += [t_shape, jax.ShapeDtypeStruct((NDEV, SUB, 2, nrow, ncol), jnp.bfloat16)]
        scratch += [pltpu.VMEM((4 * CH, ncol), jnp.float32), strided, pltpu.VMEM((NDEV, SUB, 2, RB, ncol), jnp.bfloat16),
                    pltpu.VMEM((NDEV, SUB, 2, nrow, ncol), jnp.bfloat16), pltpu.VMEM((2, NDEV, nrow, ncol), jnp.bfloat16),
                    sems, sems, pltpu.SemaphoreType.DMA((nblk,)), pltpu.SemaphoreType.DMA, pltpu.SemaphoreType.DMA((2,))]
    return pl.pallas_call(
        functools.partial(update_kernel, do_c, do_a, outgoing, nrow, ncol),
        in_specs=in_specs,
        out_specs=[hbm] * len(outs),
        out_shape=outs,
        scratch_shapes=scratch,
        compiler_params=pltpu.CompilerParams(collective_id=cid, has_side_effects=True, vmem_limit_bytes=VMEM_LIMIT),
        name="update",
    )(*args)


def solution(mesh):
    row_spec = P(ALL_ROWS, None, None)
    mask_spec = P(ALL_ROWS, None)

    def local_stack(pair_rep, pair_mask, norm_in, norm_out, w_ab, w_gate, w_out):
        mask_f = pair_mask.astype(jnp.float32)[:, None, :]
        norm_in = norm_in.astype(jnp.float32)[..., None]
        norm_out = norm_out.astype(jnp.float32)[..., None]
        w_ab = jnp.swapaxes(w_ab, -1, -2)
        w_gate = jnp.swapaxes(w_gate, -1, -2)
        w_out = jnp.swapaxes(w_out, -1, -2)
        n_layers = w_ab.shape[0]

        def cw(l, u):
            return (norm_in[l, u, 0], norm_in[l, u, 1], norm_out[l, u, 0], norm_out[l, u, 1], w_gate[l, u], w_out[l, u])

        def aw(l, u):
            return (norm_in[l, u, 0], norm_in[l, u, 1], w_ab[l, u])

        def to_incoming(l, z, t):
            z, _, t, _ = update_call(True, True, False, 1, z, t, mask_f, cw(l, 0), aw(l, 1))
            return z, t

        def body(l, state):
            z, t = to_incoming(l, *state)
            z, _, t, _ = update_call(True, True, True, 2, z, t, mask_f, cw(l, 1), aw(l + 1, 0))
            return z, t

        z = jnp.swapaxes(pair_rep, 1, 2)
        t, _ = update_call(False, True, True, 0, z, None, mask_f, None, aw(0, 0))
        z, t = lax.fori_loop(0, n_layers - 1, body, (z, t))
        z, t = to_incoming(n_layers - 1, z, t)
        z, _ = update_call(True, False, False, 3, z, t, mask_f, cw(n_layers - 1, 1), None)
        return jnp.swapaxes(z, 1, 2)

    return jax.shard_map(local_stack, mesh=mesh, in_specs=(row_spec, mask_spec, P(), P(), P(), P(), P()), out_specs=row_spec, check_vma=False)
```

time: 9580 us -> 5480 us (0.57)
  Pallas kernels: 0 us -> 5370 us
  blocking collectives: 3520 us -> 0 us
  local copies, waits for them, and re-layouts: 1680 us -> 98.1 us
  waiting for transfers between devices: 1570 us -> 0 us
  other arithmetic: 1510 us -> 1.65 us
  matrix products: 1230 us -> 0 us
    pallas_call x0 -> x13, Pallas kernels: none -> 5370 us  [update_call(): pl.pallas_call(functools.partial(update_kernel, do_c, do_a, outgoing, nro...]
    all_to_all x12 -> x0, blocking collectives: 3520 us -> none  [tri_update(): ab_cols = lax.all_to_all(ab_rows, ROW_AXES, 1, 2, tiled=True)]
    all_to_all x12 -> x0, waiting for transfers between devices: 1570 us -> none  [tri_update(): tri_rows = lax.all_to_all(tri_full, ROW_AXES, 1, 0, tiled=True)]
    dot_general x48 -> x0, matrix products: 1230 us -> none  [the longest x12 479 us: row_inputs(): jnp.einsum('de,ikd->eik', w_ab, x_ln, preferred_element_type=jnp.float32)]
    convert_element_type x29 -> x1, other arithmetic: 1200 us -> 0.94 us  [local_stack(): mask_f = pair_mask.astype(jnp.float32)[:, None, :]]
    slice x36 -> x0, local copies, waits for them, and re-layouts: 1060 us -> none  [the longest x12 833 us: row_inputs(): proj_four[:, 1]]
    convert_element_type x51 -> x0, local copies, waits for them, and re-layouts: 371 us -> none  [the longest x12 280 us: tri_update(): jnp.einsum(einsum_form, ab_cols[0], ab_cols[1], preferred_element_type=jn...]
    reduce_sum x37 -> x0, other arithmetic: 311 us -> none  [the longest x24 222 us: layer_norm(): var_val = jnp.mean(centered * centered, axis=norm_axis, keepdims=True)]
  transfers between devices with their start and end apart: 12 -> 0, of which waited for: 12 -> 0; matrix products, arithmetic and copies ran while one was open for 2% -> 0% of each run, Pallas kernels for 0% -> 0%
where the time goes in v2:
time: 5480 us; the launch traced here: 5470 us
  Pallas kernels  5370 us (98%)
  local copies, waits for them, and re-layouts  98.1 us (2%)
    pallas_call x13, Pallas kernels, update_call(): pl.pallas_call(functools.partial(update_kernel, do_c, do_a, outgoing, nro...  5370 us

profile of v2, /device:TPU:0, one launch (start us, length us, event | category | flops | bytes accessed | tf_op | source)
XLA Modules:
  0.0 5472.4 jit_solution(12987606620844485591)
XLA Ops:
  0.7 0.7 copy.22.refs_2_
  2.2 1.9 copy.21
  4.8 0.9 convert_element_type.2
  5.9 17.6 copy.20
  23.5 321.9 %update.19 = (bf16[8,16,80,640]{3,2,1,0:T(8,128)(2,1)}, bf16[8,16,2,80,640]{4,3,2,1,0:T(8,128)(2,1)}) custom-call(bf16[80,128,640]{2,1,0:T(8,128)(2,1)} %bitcast.77, f32[80,1,640]{2,1,0:T(1,128)S(1)} %broadcast_in_dim.15.refs_1_.refs_8_, f32[128,1]{1,0:T(8,128)} %copy.22.refs_2_, f32[128,1]{1,0:T(8,128)} %copy.23.refs_3_, ...), custom_call_target="tpu_custom_call" | custom-call | tf_op jit(solution)/shard_map/update/pallas_call | solution.py:232
  345.4 1.9 copy.24
  347.3 2.0 copy.25
  349.2 4494.1 %while.17 = (s32[]{:T(128)}, bf16[80,128,640]{2,1,0:T(8,128)(2,1)}, bf16[8,16,80,640]{3,2,1,0:T(8,128)(2,1)}, f32[6,2,2,128,1]{3,4,2,1,0:T(1,128)S(1)}, f32[6,2,...) while((s32[]{:T(128)}, bf16[80,128,640]{2,1,0:T(8,128)(2,1)}, ...), condition=%wide.region_1.0_spmd, body=%wide.region_0.0_spmd.sunk | while | flops 5 | bytes 807091 | solution.py:273
  349.3 0.7 copy.51.refs_9_.refs_2_
  350.0 0.7 copy.52.refs_10_.refs_3_
  351.5 0.7 copy.48.refs_3_
  354.4 1.5 dynamic-slice_bitcast_fusion.8
  355.9 444.8 %update.22 = (bf16[80,128,640]{2,1,0:T(8,128)(2,1)}, bf16[8,16,80,640]{3,2,1,0:T(8,128)(2,1)}, bf16[8,16,80,640]{3,2,1,0:T(8,128)(2,1)}, bf16[8,16,2,80,640]{4,3,2,1,0:T(8,128)(2,1)}) custom-call(bf16[80,128,640]{2,1,0:T(8,128)(2,1)} %get-tuple-element.410.refs_0_, bf16[8,16,80,640]{3,2,1,0:T(8,128)(2,1)} %get-tuple-element.411.refs_1_, ...), custom_call_target="tpu_custom_call" | custom-call | tf_op jit(solution)/shard_map/while/body/eval_jaxpr/update/pallas_call | solution.py:232
  800.7 0.7 copy.53.refs_4_
  801.4 0.7 copy.54.refs_5_
  802.9 0.7 copy.56.refs_10_
  803.6 444.4 %update.23 = (bf16[80,128,640]{2,1,0:T(8,128)(2,1)}, bf16[8,16,80,640]{3,2,1,0:T(8,128)(2,1)}, bf16[8,16,80,640]{3,2,1,0:T(8,128)(2,1)}, bf16[8,16,2,80,640]{4,3,2,1,0:T(8,128)(2,1)}) custom-call(bf16[80,128,640]{2,1,0:T(8,128)(2,1)} %get-tuple-element.386.refs_0_, bf16[8,16,80,640]{3,2,1,0:T(8,128)(2,1)} %get-tuple-element.387.refs_1_, ...), custom_call_target="tpu_custom_call" | custom-call | tf_op jit(solution)/shard_map/while/body/eval_jaxpr/update/pallas_call | solution.py:232
  1248.1 0.7 copy.51.refs_9_.refs_2_
  1248.8 0.7 copy.52.refs_10_.refs_3_
  1250.3 0.7 copy.48.refs_3_
  1251.0 0.7 copy.49.refs_4_
  1253.2 1.5 dynamic-slice_bitcast_fusion.8
  1254.7 444.9 %update.22 = (bf16[80,128,640]{2,1,0:T(8,128)(2,1)}, bf16[8,16,80,640]{3,2,1,0:T(8,128)(2,1)}, bf16[8,16,80,640]{3,2,1,0:T(8,128)(2,1)}, bf16[8,16,2,80,640]{4,3,2,1,0:T(8,128)(2,1)}) custom-call(bf16[80,128,640]{2,1,0:T(8,128)(2,1)} %get-tuple-element.410.refs_0_, bf16[8,16,80,640]{3,2,1,0:T(8,128)(2,1)} %get-tuple-element.411.refs_1_, ...), custom_call_target="tpu_custom_call" | custom-call | tf_op jit(solution)/shard_map/while/body/eval_jaxpr/update/pallas_call | solution.py:232
  1699.5 0.7 copy.53.refs_4_
  1700.3 0.7 copy.54.refs_5_
  1701.7 0.7 copy.56.refs_10_
  1702.5 444.4 %update.23 = (bf16[80,128,640]{2,1,0:T(8,128)(2,1)}, bf16[8,16,80,640]{3,2,1,0:T(8,128)(2,1)}, bf16[8,16,80,640]{3,2,1,0:T(8,128)(2,1)}, bf16[8,16,2,80,640]{4,3,2,1,0:T(8,128)(2,1)}) custom-call(bf16[80,128,640]{2,1,0:T(8,128)(2,1)} %get-tuple-element.386.refs_0_, bf16[8,16,80,640]{3,2,1,0:T(8,128)(2,1)} %get-tuple-element.387.refs_1_, ...), custom_call_target="tpu_custom_call" | custom-call | tf_op jit(solution)/shard_map/while/body/eval_jaxpr/update/pallas_call | solution.py:232
  2146.9 0.7 copy.51.refs_9_.refs_2_
  2147.7 0.7 copy.52.refs_10_.refs_3_
  2149.1 0.7 copy.48.refs_3_
  2149.9 0.7 copy.49.refs_4_
  2152.0 1.5 dynamic-slice_bitcast_fusion.8
  2153.5 444.9 %update.22 = (bf16[80,128,640]{2,1,0:T(8,128)(2,1)}, bf16[8,16,80,640]{3,2,1,0:T(8,128)(2,1)}, bf16[8,16,80,640]{3,2,1,0:T(8,128)(2,1)}, bf16[8,16,2,80,640]{4,3,2,1,0:T(8,128)(2,1)}) custom-call(bf16[80,128,640]{2,1,0:T(8,128)(2,1)} %get-tuple-element.410.refs_0_, bf16[8,16,80,640]{3,2,1,0:T(8,128)(2,1)} %get-tuple-element.411.refs_1_, ...), custom_call_target="tpu_custom_call" | custom-call | tf_op jit(solution)/shard_map/while/body/eval_jaxpr/update/pallas_call | solution.py:232
  2598.4 0.7 copy.53.refs_4_
  2599.1 0.7 copy.54.refs_5_
  2600.5 0.7 copy.56.refs_10_
  2601.3 444.4 %update.23 = (bf16[80,128,640]{2,1,0:T(8,128)(2,1)}, bf16[8,16,80,640]{3,2,1,0:T(8,128)(2,1)}, bf16[8,16,80,640]{3,2,1,0:T(8,128)(2,1)}, bf16[8,16,2,80,640]{4,3,2,1,0:T(8,128)(2,1)}) custom-call(bf16[80,128,640]{2,1,0:T(8,128)(2,1)} %get-tuple-element.386.refs_0_, bf16[8,16,80,640]{3,2,1,0:T(8,128)(2,1)} %get-tuple-element.387.refs_1_, ...), custom_call_target="tpu_custom_call" | custom-call | tf_op jit(solution)/shard_map/while/body/eval_jaxpr/update/pallas_call | solution.py:232
  3045.7 0.7 copy.51.refs_9_.refs_2_
  3046.5 0.7 copy.52.refs_10_.refs_3_
  3047.9 0.7 copy.48.refs_3_
  3050.9 1.5 dynamic-slice_bitcast_fusion.8
  3052.3 444.8 %update.22 = (bf16[80,128,640]{2,1,0:T(8,128)(2,1)}, bf16[8,16,80,640]{3,2,1,0:T(8,128)(2,1)}, bf16[8,16,80,640]{3,2,1,0:T(8,128)(2,1)}, bf16[8,16,2,80,640]{4,3,2,1,0:T(8,128)(2,1)}) custom-call(bf16[80,128,640]{2,1,0:T(8,128)(2,1)} %get-tuple-element.410.refs_0_, bf16[8,16,80,640]{3,2,1,0:T(8,128)(2,1)} %get-tuple-element.411.refs_1_, ...), custom_call_target="tpu_custom_call" | custom-call | tf_op jit(solution)/shard_map/while/body/eval_jaxpr/update/pallas_call | solution.py:232
  3497.2 0.7 copy.53.refs_4_
  3497.9 0.7 copy.54.refs_5_
  3499.4 0.7 copy.56.refs_10_
  3500.1 444.4 %update.23 = (bf16[80,128,640]{2,1,0:T(8,128)(2,1)}, bf16[8,16,80,640]{3,2,1,0:T(8,128)(2,1)}, bf16[8,16,80,640]{3,2,1,0:T(8,128)(2,1)}, bf16[8,16,2,80,640]{4,3,2,1,0:T(8,128)(2,1)}) custom-call(bf16[80,128,640]{2,1,0:T(8,128)(2,1)} %get-tuple-element.386.refs_0_, bf16[8,16,80,640]{3,2,1,0:T(8,128)(2,1)} %get-tuple-element.387.refs_1_, ...), custom_call_target="tpu_custom_call" | custom-call | tf_op jit(solution)/shard_map/while/body/eval_jaxpr/update/pallas_call | solution.py:232
  3944.6 0.7 copy.51.refs_9_.refs_2_
  3945.3 0.7 copy.52.refs_10_.refs_3_
  3946.8 0.7 copy.48.refs_3_
  3949.7 1.5 dynamic-slice_bitcast_fusion.8
  3951.1 444.8 %update.22 = (bf16[80,128,640]{2,1,0:T(8,128)(2,1)}, bf16[8,16,80,640]{3,2,1,0:T(8,128)(2,1)}, bf16[8,16,80,640]{3,2,1,0:T(8,128)(2,1)}, bf16[8,16,2,80,640]{4,3,2,1,0:T(8,128)(2,1)}) custom-call(bf16[80,128,640]{2,1,0:T(8,128)(2,1)} %get-tuple-element.410.refs_0_, bf16[8,16,80,640]{3,2,1,0:T(8,128)(2,1)} %get-tuple-element.411.refs_1_, ...), custom_call_target="tpu_custom_call" | custom-call | tf_op jit(solution)/shard_map/while/body/eval_jaxpr/update/pallas_call | solution.py:232
  4396.0 0.7 copy.53.refs_4_
  4396.7 0.7 copy.54.refs_5_
  4398.2 0.7 copy.56.refs_10_
  4398.9 444.4 %update.23 = (bf16[80,128,640]{2,1,0:T(8,128)(2,1)}, bf16[8,16,80,640]{3,2,1,0:T(8,128)(2,1)}, bf16[8,16,80,640]{3,2,1,0:T(8,128)(2,1)}, bf16[8,16,2,80,640]{4,3,2,1,0:T(8,128)(2,1)}) custom-call(bf16[80,128,640]{2,1,0:T(8,128)(2,1)} %get-tuple-element.386.refs_0_, bf16[8,16,80,640]{3,2,1,0:T(8,128)(2,1)} %get-tuple-element.387.refs_1_, ...), custom_call_target="tpu_custom_call" | custom-call | tf_op jit(solution)/shard_map/while/body/eval_jaxpr/update/pallas_call | solution.py:232
  4843.4 0.7 copy.30.refs_9_.refs_2_
  4844.1 0.7 copy.31.refs_10_.refs_3_
  4845.6 0.7 copy.27.refs_3_
  4846.3 1.5 slice_bitcast_fusion.2
  4847.8 0.7 copy.28.refs_4_
  4849.2 444.8 %update.20 = (bf16[80,128,640]{2,1,0:T(8,128)(2,1)}, bf16[8,16,80,640]{3,2,1,0:T(8,128)(2,1)}, bf16[8,16,80,640]{3,2,1,0:T(8,128)(2,1)}, bf16[8,16,2,80,640]{4,3,2,1,0:T(8,128)(2,1)}) custom-call(bf16[80,128,640]{2,1,0:T(8,128)(2,1)} %get-tuple-element.237.refs_0_, bf16[8,16,80,640]{3,2,1,0:T(8,128)(2,1)} %get-tuple-element.238.refs_1_, ...), custom_call_target="tpu_custom_call" | custom-call | tf_op jit(solution)/shard_map/update/pallas_call | solution.py:232
  5294.1 0.7 copy.34.refs_4_
  5295.6 159.3 %update.21 = (bf16[80,128,640]{2,1,0:T(8,128)(2,1)}, bf16[8,16,80,640]{3,2,1,0:T(8,128)(2,1)}) custom-call(bf16[80,128,640]{2,1,0:T(8,128)(2,1)} %get-tuple-element.239.refs_0_, bf16[8,16,80,640]{3,2,1,0:T(8,128)(2,1)} %get-tuple-element.240.refs_1_, f32[128,1]{1,0:T(8,128)} %copy.30.refs_9_.refs_2_, f32[128,1]{1,0:T(8,128)} %copy.31.refs_10_.refs_3_, ...), custom_call_target="tpu_custom_call" | custom-call | tf_op jit(solution)/shard_map/update/pallas_call | solution.py:232
  5454.9 17.5 copy.36
  (40 shorter events, 21.3 us)
Async XLA Ops:
  23.5 325.8 %copy-start = (bf16[6,2,2,128]{3,2,1,0:T(2,128)(2,1)S(1)}, bf16[6,2,2,128]{3,2,1,0:T(2,128)(2,1)}, u32[]{:S(2)}) copy-start(bf16[6,2,2,128]{3,2,1,0:T(2,128)(2,1)} %param.12) | copy-start | bytes 18436

commit v3 on v2

--- a/solution.py
+++ b/solution.py
@@ -30,6 +30,10 @@
     return 0.5 * jnp.tanh(0.5 * vals) + 0.5
 
 
+def first_and_rest(do_c):
+    return (4, ((4, 4), (8, 4), (12, 2), (14, 2))) if do_c else (8, ((8, 4), (12, 2), (14, 2)))
+
+
 def update_kernel(do_c, do_a, outgoing, nrow, ncol, *refs):
     refs = list(refs)
 
@@ -40,9 +44,10 @@
 
     z_ref, = take(1)
     if do_c:
-        t_ref, gip_ref, sip_ref, go_ref, so_ref, wg_ref, wo_ref = take(7)
-    if do_a:
-        m_ref, gi_ref, si_ref, wab_ref = take(4)
+        t_ref, = take(1)
+    if do_a:
+        m_ref, = take(1)
+    v_ref, w_ref = take(2)
     if do_c:
         zo_ref, tr_ref = take(2)
     if do_a:
@@ -51,7 +56,7 @@
     if do_c:
         o_ref, g_ref, y_ref, tblk, s_t, r_t, l_t = take(7)
     if do_a:
-        p_ref, scr_b, abblk, recv, tst, s_ab, r_ab, l_ab, l_st, l_tn = take(10)
+        p_ref, scr_b, abblk, recv, tst, s_ab, r_ab, l_ab, l_st, l_tn, s_rest, r_rest, l_rest = take(13)
 
     y_id = lax.axis_index("dap2")
     xc_id = lax.axis_index("dap")
@@ -59,7 +64,7 @@
     x_id, c_id = xc_id // 2, xc_id % 2
     me = y_id * 4 + xc_id
     nblk = nrow // RB
-    nlane = ncol // LANES
+    first, rest = first_and_rest(do_c)
 
     def peer(d):
         py, px, pc = (y_id + d // 4) % 2, (x_id + (d // 2) % 2) % 2, (c_id + d % 2) % 2
@@ -77,11 +82,20 @@
     def ab_copy(r, d):
         dev, num = peer(d)
         return pltpu.make_async_remote_copy(
-            src_ref=ab_ref.at[num, :, :, rows(r)], dst_ref=recv.at[me, :, :, rows(r)],
+            src_ref=ab_ref.at[num, pl.ds(0, first), :, rows(r)], dst_ref=recv.at[me, pl.ds(0, first), :, rows(r)],
             send_sem=s_ab.at[r, d], recv_sem=r_ab.at[r, d], device_id=dev, device_id_type=MESH)
 
     def own_ab(r):
-        return pltpu.make_async_copy(ab_ref.at[me, :, :, rows(r)], recv.at[me, :, :, rows(r)], l_ab.at[r])
+        return pltpu.make_async_copy(ab_ref.at[me, pl.ds(0, first), :, rows(r)], recv.at[me, pl.ds(0, first), :, rows(r)], l_ab.at[r])
+
+    def rest_copy(g, d):
+        dev, num = peer(d)
+        return pltpu.make_async_remote_copy(
+            src_ref=ab_ref.at[num, pl.ds(*rest[g])], dst_ref=recv.at[me, pl.ds(*rest[g])],
+            send_sem=s_rest.at[g, d], recv_sem=r_rest.at[g, d], device_id=dev, device_id_type=MESH)
+
+    def own_rest():
+        return pltpu.make_async_copy(ab_ref.at[me, pl.ds(first, SUB - first)], recv.at[me, pl.ds(first, SUB - first)], l_rest)
 
     def stage_ab(r):
         return pltpu.make_async_copy(abblk, ab_ref.at[:, :, :, rows(r)], l_st)
@@ -112,17 +126,17 @@
     def one_row(r, i):
         if do_c:
             for q, ln in enumerate(chunks):
-                x_ref[:, ln] = norm_cols(zbuf[i, :, ln].astype(jnp.float32), gip_ref[...], sip_ref[...]).astype(jnp.bfloat16)
-                y_ref[:, ln] = norm_cols(scr[q, pl.ds(i, CH, stride=RB), :], go_ref[...], so_ref[...]).astype(jnp.bfloat16)
-            g_ref[...] = jnp.dot(wg_ref[...], x_ref[...], preferred_element_type=jnp.float32)
-            o_ref[...] = jnp.dot(wo_ref[...], y_ref[...], preferred_element_type=jnp.float32)
+                x_ref[:, ln] = norm_cols(zbuf[i, :, ln].astype(jnp.float32), v_ref[:, 0:1], v_ref[:, 1:2]).astype(jnp.bfloat16)
+                y_ref[:, ln] = norm_cols(scr[q, pl.ds(i, CH, stride=RB), :], v_ref[:, 2:3], v_ref[:, 3:4]).astype(jnp.bfloat16)
+            g_ref[...] = jnp.dot(w_ref[pl.ds(0, CH), :], x_ref[...], preferred_element_type=jnp.float32)
+            o_ref[...] = jnp.dot(w_ref[pl.ds(CH, CH), :], y_ref[...], preferred_element_type=jnp.float32)
             for q, ln in enumerate(chunks):
                 new_z = zbuf[i, :, ln].astype(jnp.float32) + sigmoid(g_ref[:, ln]) * o_ref[:, ln]
                 zbuf[i, :, ln] = new_z.astype(jnp.bfloat16)
         if do_a:
             for q, ln in enumerate(chunks):
-                x_ref[:, ln] = norm_cols(zbuf[i, :, ln].astype(jnp.float32), gi_ref[...], si_ref[...]).astype(jnp.bfloat16)
-            p_ref[...] = jnp.dot(wab_ref[...], x_ref[...], preferred_element_type=jnp.float32)
+                x_ref[:, ln] = norm_cols(zbuf[i, :, ln].astype(jnp.float32), v_ref[:, 4:5], v_ref[:, 5:6]).astype(jnp.bfloat16)
+            p_ref[...] = jnp.dot(w_ref[pl.ds(2 * CH, 4 * CH), :], x_ref[...], preferred_element_type=jnp.float32)
             for q, ln in enumerate(chunks):
                 keep = m_ref[r * RB + i, :, ln]
                 scr[q, pl.ds(i, CH, stride=RB), :] = keep * sigmoid(p_ref[pl.ds(CH, CH), ln]) * p_ref[pl.ds(0, CH), ln]
@@ -166,6 +180,11 @@
     lax.fori_loop(0, nblk, block_step, 0)
 
     if do_a:
+        for g in range(len(rest)):
+            for d in ORDER:
+                rest_copy(g, d).start()
+        own_rest().start()
+
         def wait_ab(r, carry):
             for d in ORDER:
                 ab_copy(r, d).wait_recv()
@@ -173,11 +192,18 @@
             return carry
 
         lax.fori_loop(0, nblk, wait_ab, 0)
+        own_rest().wait()
 
         def put_t(ch):
             return pltpu.make_async_copy(tst.at[ch % 2], tn_ref.at[:, ch], l_tn.at[ch % 2])
 
         def chan_step(ch, carry):
+            for g in range(len(rest)):
+                @pl.when(ch == rest[g][0])
+                def _(g=g):
+                    for d in ORDER:
+                        rest_copy(g, d).wait_recv()
+
             a_val = recv[:, ch, 0].reshape(NDEV * nrow, ncol)
             b_val = recv[:, ch, 1].reshape(NDEV * nrow, ncol)
             dims = (((1,), (1,)), ((), ())) if outgoing else (((0,), (0,)), ((), ()))
@@ -204,9 +230,13 @@
         return carry
 
     lax.fori_loop(0, nblk, drain, 0)
-
-
-def update_call(do_c, do_a, outgoing, cid, z, t, mask, cw, aw):
+    if do_a:
+        for g in range(len(rest)):
+            for d in ORDER:
+                rest_copy(g, d).wait_send()
+
+
+def update_call(do_c, do_a, outgoing, cid, z, t, mask, vecs, mats):
     nrow, _, ncol = z.shape
     nblk = nrow // RB
     hbm = pl.BlockSpec(memory_space=pl.ANY)
@@ -217,18 +247,22 @@
     args, in_specs, outs = [z], [hbm], []
     scratch = [pltpu.VMEM((RB, CH, ncol), jnp.bfloat16), strided, pltpu.VMEM((CH, ncol), jnp.bfloat16), pltpu.SemaphoreType.DMA]
     if do_c:
-        args += [t, *cw]
-        in_specs += [hbm] + [vmem] * len(cw)
+        args.append(t)
+        in_specs.append(hbm)
         outs += [jax.ShapeDtypeStruct(z.shape, jnp.bfloat16), t_shape]
         scratch += [pltpu.VMEM((CH, ncol), jnp.float32), pltpu.VMEM((CH, ncol), jnp.float32), pltpu.VMEM((CH, ncol), jnp.bfloat16),
                     pltpu.VMEM((NDEV, SUB, RB, ncol), jnp.bfloat16), sems, sems, pltpu.SemaphoreType.DMA((NDEV,))]
     if do_a:
-        args += [mask, *aw]
-        in_specs += [vmem] * (1 + len(aw))
+        args.append(mask)
+        in_specs.append(vmem)
+        nrest = len(first_and_rest(do_c)[1])
+        rsems = pltpu.SemaphoreType.DMA((nrest, NDEV))
         outs += [t_shape, jax.ShapeDtypeStruct((NDEV, SUB, 2, nrow, ncol), jnp.bfloat16)]
         scratch += [pltpu.VMEM((4 * CH, ncol), jnp.float32), strided, pltpu.VMEM((NDEV, SUB, 2, RB, ncol), jnp.bfloat16),
                     pltpu.VMEM((NDEV, SUB, 2, nrow, ncol), jnp.bfloat16), pltpu.VMEM((2, NDEV, nrow, ncol), jnp.bfloat16),
-                    sems, sems, pltpu.SemaphoreType.DMA((nblk,)), pltpu.SemaphoreType.DMA, pltpu.SemaphoreType.DMA((2,))]
+                    sems, sems, pltpu.SemaphoreType.DMA((nblk,)), pltpu.SemaphoreType.DMA, pltpu.SemaphoreType.DMA((2,)), rsems, rsems, pltpu.SemaphoreType.DMA]
+    args += [vecs, mats]
+    in_specs += [vmem, vmem]
     return pl.pallas_call(
         functools.partial(update_kernel, do_c, do_a, outgoing, nrow, ncol),
         in_specs=in_specs,
@@ -246,33 +280,32 @@
 
     def local_stack(pair_rep, pair_mask, norm_in, norm_out, w_ab, w_gate, w_out):
         mask_f = pair_mask.astype(jnp.float32)[:, None, :]
-        norm_in = norm_in.astype(jnp.float32)[..., None]
-        norm_out = norm_out.astype(jnp.float32)[..., None]
-        w_ab = jnp.swapaxes(w_ab, -1, -2)
-        w_gate = jnp.swapaxes(w_gate, -1, -2)
-        w_out = jnp.swapaxes(w_out, -1, -2)
         n_layers = w_ab.shape[0]
-
-        def cw(l, u):
-            return (norm_in[l, u, 0], norm_in[l, u, 1], norm_out[l, u, 0], norm_out[l, u, 1], w_gate[l, u], w_out[l, u])
-
-        def aw(l, u):
-            return (norm_in[l, u, 0], norm_in[l, u, 1], w_ab[l, u])
+        n_upd = 2 * n_layers
+        n_in = norm_in.astype(jnp.float32).reshape(n_upd, 2, CH)
+        n_out = norm_out.astype(jnp.float32).reshape(n_upd, 2, CH)
+        n_next = jnp.roll(n_in, -1, axis=0)
+        vecs = jnp.stack([n_in[:, 0], n_in[:, 1], n_out[:, 0], n_out[:, 1], n_next[:, 0], n_next[:, 1]], axis=-1)
+
+        def rows_of(w):
+            return jnp.swapaxes(w.reshape(n_upd, *w.shape[2:]), 1, 2)
+
+        mats = jnp.concatenate([rows_of(w_gate), rows_of(w_out), jnp.roll(rows_of(w_ab), -1, axis=0)], axis=1)
 
         def to_incoming(l, z, t):
-            z, _, t, _ = update_call(True, True, False, 1, z, t, mask_f, cw(l, 0), aw(l, 1))
+            z, _, t, _ = update_call(True, True, False, 1, z, t, mask_f, vecs[2 * l], mats[2 * l])
             return z, t
 
         def body(l, state):
             z, t = to_incoming(l, *state)
-            z, _, t, _ = update_call(True, True, True, 2, z, t, mask_f, cw(l, 1), aw(l + 1, 0))
+            z, _, t, _ = update_call(True, True, True, 2, z, t, mask_f, vecs[2 * l + 1], mats[2 * l + 1])
             return z, t
 
         z = jnp.swapaxes(pair_rep, 1, 2)
-        t, _ = update_call(False, True, True, 0, z, None, mask_f, None, aw(0, 0))
+        t, _ = update_call(False, True, True, 0, z, None, mask_f, vecs[n_upd - 1], mats[n_upd - 1])
         z, t = lax.fori_loop(0, n_layers - 1, body, (z, t))
         z, t = to_incoming(n_layers - 1, z, t)
-        z, _ = update_call(True, False, False, 3, z, t, mask_f, cw(n_layers - 1, 1), None)
+        z, _ = update_call(True, False, False, 3, z, t, mask_f, vecs[n_upd - 1], mats[n_upd - 1])
         return jnp.swapaxes(z, 1, 2)
 
     return jax.shard_map(local_stack, mesh=mesh, in_specs=(row_spec, mask_spec, P(), P(), P(), P(), P()), out_specs=row_spec, check_vma=False)

time: 5480 us -> 5280 us (0.964)
  Pallas kernels: 5370 us -> 5210 us
    pallas_call x13, Pallas kernels: 5370 us -> 5210 us  [update_call(): pl.pallas_call(functools.partial(update_kernel, do_c, do_a, outgoing, nro...]
where the time goes in v3:
time: 5280 us
  Pallas kernels  5210 us (99%)
  local copies, waits for them, and re-layouts  60.3 us (1%)
    pallas_call x13, Pallas kernels, update_call(): pl.pallas_call(functools.partial(update_kernel, do_c, do_a, outgoing, nro...  5210 us

profile of v3, /device:TPU:0, one launch (start us, length us, event | category | flops | bytes accessed | tf_op | source)
XLA Modules:
  0.0 5275.9 jit_solution(2241553203015404928)
XLA Ops:
  0.0 0.7 bitcast_convert_fusion.1
  0.7 0.7 bitcast_convert_fusion
  1.4 0.1 stack.3
  1.5 0.9 convert_element_type.2
  2.5 0.1 broadcast_in_dim.3.refs_1_.refs_2_
  2.6 1.2 copy.44
  3.8 1.9 copy.45
  5.8 0.3 copy.43
  6.1 0.0 copy-start.1
  6.1 0.7 slice_bitcast_fusion.2
  6.8 1.9 copy.46
  8.7 0.1 slice.71
  8.8 1.2 maximum_maximum_fusion
  10.0 0.0 copy-start
  10.0 1.4 copy-done
  11.4 0.8 slice_bitcast_fusion
  12.2 17.6 copy.42
  29.8 0.0 copy-done.1
  29.8 309.2 %update.19 = (bf16[8,16,80,640]{3,2,1,0:T(8,128)(2,1)}, bf16[8,16,2,80,640]{4,3,2,1,0:T(8,128)(2,1)}) custom-call(bf16[80,128,640]{2,1,0:T(8,128)(2,1)} %bitcast.49, f32[80,1,640]{2,1,0:T(1,128)S(1)} %broadcast_in_dim.3.refs_1_.refs_2_, f32[128,6]{1,0:T(8,128)} %get-tuple-element.201.refs_2_, bf16[768,128]{1,0:T(8,128)(2,1)} %get-tuple-element.199.refs_3_), custom_call_target="tpu_custom_call" | custom-call | tf_op jit(solution)/shard_map/update/pallas_call | solution.py:266
  339.0 4327.4 %while.17 = (s32[]{:T(128)}, bf16[80,128,640]{2,1,0:T(8,128)(2,1)}, bf16[8,16,80,640]{3,2,1,0:T(8,128)(2,1)}, f32[12,128,6]{2,1,0:T(8,128)}, bf16[12,768,128]{2,...) while((s32[]{:T(128)}, bf16[80,128,640]{2,1,0:T(8,128)(2,1)}, ...), condition=%wide.region_1.2_spmd, body=%wide.region_0.1_spmd.sunk | while | flops 10 | bytes 798937 | solution.py:306
  339.0 1.5 dynamic-slice_bitcast_fusion.6
  340.5 1.8 dynamic-slice_bitcast_fusion.7
  342.3 431.2 %update.22 = (bf16[80,128,640]{2,1,0:T(8,128)(2,1)}, bf16[8,16,80,640]{3,2,1,0:T(8,128)(2,1)}, bf16[8,16,80,640]{3,2,1,0:T(8,128)(2,1)}, bf16[8,16,2,80,640]{4,3,2,1,0:T(8,128)(2,1)}) custom-call(bf16[80,128,640]{2,1,0:T(8,128)(2,1)} %get-tuple-element.275.refs_0_, bf16[8,16,80,640]{3,2,1,0:T(8,128)(2,1)} %get-tuple-element.276.refs_1_, ...), custom_call_target="tpu_custom_call" | custom-call | tf_op jit(solution)/shard_map/while/body/eval_jaxpr/update/pallas_call | solution.py:266
  773.5 430.9 %update.23 = (bf16[80,128,640]{2,1,0:T(8,128)(2,1)}, bf16[8,16,80,640]{3,2,1,0:T(8,128)(2,1)}, bf16[8,16,80,640]{3,2,1,0:T(8,128)(2,1)}, bf16[8,16,2,80,640]{4,3,2,1,0:T(8,128)(2,1)}) custom-call(bf16[80,128,640]{2,1,0:T(8,128)(2,1)} %get-tuple-element.257.refs_0_, bf16[8,16,80,640]{3,2,1,0:T(8,128)(2,1)} %get-tuple-element.258.refs_1_, ...), custom_call_target="tpu_custom_call" | custom-call | tf_op jit(solution)/shard_map/while/body/eval_jaxpr/update/pallas_call | solution.py:266
  1204.4 1.5 dynamic-slice_bitcast_fusion.6
  1206.0 1.8 dynamic-slice_bitcast_fusion.7
  1207.8 431.2 %update.22 = (bf16[80,128,640]{2,1,0:T(8,128)(2,1)}, bf16[8,16,80,640]{3,2,1,0:T(8,128)(2,1)}, bf16[8,16,80,640]{3,2,1,0:T(8,128)(2,1)}, bf16[8,16,2,80,640]{4,3,2,1,0:T(8,128)(2,1)}) custom-call(bf16[80,128,640]{2,1,0:T(8,128)(2,1)} %get-tuple-element.275.refs_0_, bf16[8,16,80,640]{3,2,1,0:T(8,128)(2,1)} %get-tuple-element.276.refs_1_, ...), custom_call_target="tpu_custom_call" | custom-call | tf_op jit(solution)/shard_map/while/body/eval_jaxpr/update/pallas_call | solution.py:266
  1639.0 430.9 %update.23 = (bf16[80,128,640]{2,1,0:T(8,128)(2,1)}, bf16[8,16,80,640]{3,2,1,0:T(8,128)(2,1)}, bf16[8,16,80,640]{3,2,1,0:T(8,128)(2,1)}, bf16[8,16,2,80,640]{4,3,2,1,0:T(8,128)(2,1)}) custom-call(bf16[80,128,640]{2,1,0:T(8,128)(2,1)} %get-tuple-element.257.refs_0_, bf16[8,16,80,640]{3,2,1,0:T(8,128)(2,1)} %get-tuple-element.258.refs_1_, ...), custom_call_target="tpu_custom_call" | custom-call | tf_op jit(solution)/shard_map/while/body/eval_jaxpr/update/pallas_call | solution.py:266
  2069.9 1.5 dynamic-slice_bitcast_fusion.6
  2071.4 1.8 dynamic-slice_bitcast_fusion.7
  2073.3 431.2 %update.22 = (bf16[80,128,640]{2,1,0:T(8,128)(2,1)}, bf16[8,16,80,640]{3,2,1,0:T(8,128)(2,1)}, bf16[8,16,80,640]{3,2,1,0:T(8,128)(2,1)}, bf16[8,16,2,80,640]{4,3,2,1,0:T(8,128)(2,1)}) custom-call(bf16[80,128,640]{2,1,0:T(8,128)(2,1)} %get-tuple-element.275.refs_0_, bf16[8,16,80,640]{3,2,1,0:T(8,128)(2,1)} %get-tuple-element.276.refs_1_, ...), custom_call_target="tpu_custom_call" | custom-call | tf_op jit(solution)/shard_map/while/body/eval_jaxpr/update/pallas_call | solution.py:266
  2504.4 430.9 %update.23 = (bf16[80,128,640]{2,1,0:T(8,128)(2,1)}, bf16[8,16,80,640]{3,2,1,0:T(8,128)(2,1)}, bf16[8,16,80,640]{3,2,1,0:T(8,128)(2,1)}, bf16[8,16,2,80,640]{4,3,2,1,0:T(8,128)(2,1)}) custom-call(bf16[80,128,640]{2,1,0:T(8,128)(2,1)} %get-tuple-element.257.refs_0_, bf16[8,16,80,640]{3,2,1,0:T(8,128)(2,1)} %get-tuple-element.258.refs_1_, ...), custom_call_target="tpu_custom_call" | custom-call | tf_op jit(solution)/shard_map/while/body/eval_jaxpr/update/pallas_call | solution.py:266
  2935.4 1.5 dynamic-slice_bitcast_fusion.6
  2936.9 1.8 dynamic-slice_bitcast_fusion.7
  2938.7 431.2 %update.22 = (bf16[80,128,640]{2,1,0:T(8,128)(2,1)}, bf16[8,16,80,640]{3,2,1,0:T(8,128)(2,1)}, bf16[8,16,80,640]{3,2,1,0:T(8,128)(2,1)}, bf16[8,16,2,80,640]{4,3,2,1,0:T(8,128)(2,1)}) custom-call(bf16[80,128,640]{2,1,0:T(8,128)(2,1)} %get-tuple-element.275.refs_0_, bf16[8,16,80,640]{3,2,1,0:T(8,128)(2,1)} %get-tuple-element.276.refs_1_, ...), custom_call_target="tpu_custom_call" | custom-call | tf_op jit(solution)/shard_map/while/body/eval_jaxpr/update/pallas_call | solution.py:266
  3369.9 430.9 %update.23 = (bf16[80,128,640]{2,1,0:T(8,128)(2,1)}, bf16[8,16,80,640]{3,2,1,0:T(8,128)(2,1)}, bf16[8,16,80,640]{3,2,1,0:T(8,128)(2,1)}, bf16[8,16,2,80,640]{4,3,2,1,0:T(8,128)(2,1)}) custom-call(bf16[80,128,640]{2,1,0:T(8,128)(2,1)} %get-tuple-element.257.refs_0_, bf16[8,16,80,640]{3,2,1,0:T(8,128)(2,1)} %get-tuple-element.258.refs_1_, ...), custom_call_target="tpu_custom_call" | custom-call | tf_op jit(solution)/shard_map/while/body/eval_jaxpr/update/pallas_call | solution.py:266
  3800.9 1.5 dynamic-slice_bitcast_fusion.6
  3802.4 1.8 dynamic-slice_bitcast_fusion.7
  3804.2 431.2 %update.22 = (bf16[80,128,640]{2,1,0:T(8,128)(2,1)}, bf16[8,16,80,640]{3,2,1,0:T(8,128)(2,1)}, bf16[8,16,80,640]{3,2,1,0:T(8,128)(2,1)}, bf16[8,16,2,80,640]{4,3,2,1,0:T(8,128)(2,1)}) custom-call(bf16[80,128,640]{2,1,0:T(8,128)(2,1)} %get-tuple-element.275.refs_0_, bf16[8,16,80,640]{3,2,1,0:T(8,128)(2,1)} %get-tuple-element.276.refs_1_, ...), custom_call_target="tpu_custom_call" | custom-call | tf_op jit(solution)/shard_map/while/body/eval_jaxpr/update/pallas_call | solution.py:266
  4235.4 430.9 %update.23 = (bf16[80,128,640]{2,1,0:T(8,128)(2,1)}, bf16[8,16,80,640]{3,2,1,0:T(8,128)(2,1)}, bf16[8,16,80,640]{3,2,1,0:T(8,128)(2,1)}, bf16[8,16,2,80,640]{4,3,2,1,0:T(8,128)(2,1)}) custom-call(bf16[80,128,640]{2,1,0:T(8,128)(2,1)} %get-tuple-element.257.refs_0_, bf16[8,16,80,640]{3,2,1,0:T(8,128)(2,1)} %get-tuple-element.258.refs_1_, ...), custom_call_target="tpu_custom_call" | custom-call | tf_op jit(solution)/shard_map/while/body/eval_jaxpr/update/pallas_call | solution.py:266
  4666.4 431.2 %update.20 = (bf16[80,128,640]{2,1,0:T(8,128)(2,1)}, bf16[8,16,80,640]{3,2,1,0:T(8,128)(2,1)}, bf16[8,16,80,640]{3,2,1,0:T(8,128)(2,1)}, bf16[8,16,2,80,640]{4,3,2,1,0:T(8,128)(2,1)}) custom-call(bf16[80,128,640]{2,1,0:T(8,128)(2,1)} %get-tuple-element.171.refs_0_, bf16[8,16,80,640]{3,2,1,0:T(8,128)(2,1)} %get-tuple-element.172.refs_1_, ...), custom_call_target="tpu_custom_call" | custom-call | tf_op jit(solution)/shard_map/update/pallas_call | solution.py:266
  5097.5 160.9 %update.21 = (bf16[80,128,640]{2,1,0:T(8,128)(2,1)}, bf16[8,16,80,640]{3,2,1,0:T(8,128)(2,1)}) custom-call(bf16[80,128,640]{2,1,0:T(8,128)(2,1)} %get-tuple-element.173.refs_0_, bf16[8,16,80,640]{3,2,1,0:T(8,128)(2,1)} %get-tuple-element.174.refs_1_, f32[128,6]{1,0:T(8,128)} %get-tuple-element.201.refs_2_, bf16[768,128]{1,0:T(8,128)(2,1)} %get-tuple-element.199.refs_3_), custom_call_target="tpu_custom_call" | custom-call | tf_op jit(solution)/shard_map/update/pallas_call | solution.py:266
  5258.5 17.5 copy.49
  (5 shorter events, 0.0 us)
Async XLA Ops:
  6.1 23.7 copy-start.1
  10.0 1.4 copy-start

commit v4 on v3

--- a/solution.py
+++ b/solution.py
@@ -31,7 +31,7 @@
 
 
 def first_and_rest(do_c):
-    return (4, ((4, 4), (8, 4), (12, 2), (14, 2))) if do_c else (8, ((8, 4), (12, 2), (14, 2)))
+    return (4, ((4, 4), (8, 4), (12, 3), (15, 1))) if do_c else (8, ((8, 4), (12, 3), (15, 1)))
 
 
 def update_kernel(do_c, do_a, outgoing, nrow, ncol, *refs):
@@ -46,17 +46,17 @@
     if do_c:
         t_ref, = take(1)
     if do_a:
-        m_ref, = take(1)
-    v_ref, w_ref = take(2)
+        m_hbm, = take(1)
+    v_hbm, w_hbm = take(2)
     if do_c:
         zo_ref, tr_ref = take(2)
     if do_a:
         tn_ref, ab_ref = take(2)
-    zbuf, scr, x_ref, l_z = take(4)
+    zbuf, scr, x_ref, l_z, v_ref, w_ref, l_par = take(7)
     if do_c:
         o_ref, g_ref, y_ref, tblk, s_t, r_t, l_t = take(7)
     if do_a:
-        p_ref, scr_b, abblk, recv, tst, s_ab, r_ab, l_ab, l_st, l_tn, s_rest, r_rest, l_rest = take(13)
+        p_ref, scr_b, abblk, recv, tst, s_ab, r_ab, l_ab, l_st, l_tn, s_rest, r_rest, l_rest, m_ref = take(14)
 
     y_id = lax.axis_index("dap2")
     xc_id = lax.axis_index("dap")
@@ -120,6 +120,13 @@
         for r in range(nblk):
             for d in ORDER:
                 t_copy(r, d).start()
+
+    params = [(v_hbm, v_ref), (w_hbm, w_ref)] + ([(m_hbm, m_ref)] if do_a else [])
+    loads = [pltpu.make_async_copy(src, dst, l_par.at[n]) for n, (src, dst) in enumerate(params)]
+    for load in loads:
+        load.start()
+    for load in loads:
+        load.wait()
 
     chunks = [pl.ds(l0, LANES) for l0 in range(0, ncol, LANES)]
 
@@ -240,12 +247,12 @@
     nrow, _, ncol = z.shape
     nblk = nrow // RB
     hbm = pl.BlockSpec(memory_space=pl.ANY)
-    vmem = pl.BlockSpec(memory_space=pltpu.VMEM)
     sems = pltpu.SemaphoreType.DMA((nblk, NDEV))
     strided = pltpu.VMEM((ncol // LANES, CH * RB, LANES), jnp.float32)
     t_shape = jax.ShapeDtypeStruct((NDEV, SUB, nrow, ncol), jnp.bfloat16)
     args, in_specs, outs = [z], [hbm], []
-    scratch = [pltpu.VMEM((RB, CH, ncol), jnp.bfloat16), strided, pltpu.VMEM((CH, ncol), jnp.bfloat16), pltpu.SemaphoreType.DMA]
+    scratch = [pltpu.VMEM((RB, CH, ncol), jnp.bfloat16), strided, pltpu.VMEM((CH, ncol), jnp.bfloat16), pltpu.SemaphoreType.DMA,
+               pltpu.VMEM(vecs.shape, vecs.dtype), pltpu.VMEM(mats.shape, mats.dtype), pltpu.SemaphoreType.DMA((3,))]
     if do_c:
         args.append(t)
         in_specs.append(hbm)
@@ -254,15 +261,15 @@
                     pltpu.VMEM((NDEV, SUB, RB, ncol), jnp.bfloat16), sems, sems, pltpu.SemaphoreType.DMA((NDEV,))]
     if do_a:
         args.append(mask)
-        in_specs.append(vmem)
+        in_specs.append(hbm)
         nrest = len(first_and_rest(do_c)[1])
         rsems = pltpu.SemaphoreType.DMA((nrest, NDEV))
         outs += [t_shape, jax.ShapeDtypeStruct((NDEV, SUB, 2, nrow, ncol), jnp.bfloat16)]
         scratch += [pltpu.VMEM((4 * CH, ncol), jnp.float32), strided, pltpu.VMEM((NDEV, SUB, 2, RB, ncol), jnp.bfloat16),
                     pltpu.VMEM((NDEV, SUB, 2, nrow, ncol), jnp.bfloat16), pltpu.VMEM((2, NDEV, nrow, ncol), jnp.bfloat16),
-                    sems, sems, pltpu.SemaphoreType.DMA((nblk,)), pltpu.SemaphoreType.DMA, pltpu.SemaphoreType.DMA((2,)), rsems, rsems, pltpu.SemaphoreType.DMA]
+                    sems, sems, pltpu.SemaphoreType.DMA((nblk,)), pltpu.SemaphoreType.DMA, pltpu.SemaphoreType.DMA((2,)), rsems, rsems, pltpu.SemaphoreType.DMA, pltpu.VMEM(mask.shape, mask.dtype)]
     args += [vecs, mats]
-    in_specs += [vmem, vmem]
+    in_specs += [hbm, hbm]
     return pl.pallas_call(
         functools.partial(update_kernel, do_c, do_a, outgoing, nrow, ncol),
         in_specs=in_specs,

time: 5280 us -> 5260 us (level)
  no operation moved by 1% of the time
where the time goes in v4:
time: 5260 us; the launch traced here: 5250 us
  Pallas kernels  5190 us (99%)
  local copies, waits for them, and re-layouts  60.3 us (1%)
    pallas_call x13, Pallas kernels, update_call(): pl.pallas_call(functools.partial(update_kernel, do_c, do_a, outgoing, nro...  5190 us

profile of v4, /device:TPU:0, one launch (start us, length us, event | category | flops | bytes accessed | tf_op | source)
XLA Modules:
  0.0 5252.9 jit_solution(16698444907984950359)
XLA Ops:
  0.0 0.7 bitcast_convert_fusion.1
  0.7 0.7 bitcast_convert_fusion
  1.4 0.1 stack.3
  1.5 0.9 convert_element_type.2
  2.5 0.1 broadcast_in_dim.3.refs_1_.refs_2_
  2.6 1.2 copy.44
  3.8 1.9 copy.45
  5.8 0.3 copy.43
  6.1 0.0 copy-start.1
  6.1 0.7 slice_bitcast_fusion.2
  6.8 1.9 copy.46
  8.7 0.1 slice.71
  8.8 1.2 maximum_maximum_fusion
  10.0 0.0 copy-start
  10.0 1.4 copy-done
  11.4 0.8 slice_bitcast_fusion
  12.2 17.6 copy.42
  29.8 0.0 copy-done.1
  29.8 308.2 %update.19 = (bf16[8,16,80,640]{3,2,1,0:T(8,128)(2,1)}, bf16[8,16,2,80,640]{4,3,2,1,0:T(8,128)(2,1)}) custom-call(bf16[80,128,640]{2,1,0:T(8,128)(2,1)} %bitcast.49, f32[80,1,640]{2,1,0:T(1,128)S(1)} %broadcast_in_dim.3.refs_1_.refs_2_, f32[128,6]{1,0:T(8,128)} %get-tuple-element.201.refs_2_, bf16[768,128]{1,0:T(8,128)(2,1)} %get-tuple-element.199.refs_3_), custom_call_target="tpu_custom_call" | custom-call | tf_op jit(solution)/shard_map/update/pallas_call | solution.py:273
  338.0 4308.0 %while.17 = (s32[]{:T(128)}, bf16[80,128,640]{2,1,0:T(8,128)(2,1)}, bf16[8,16,80,640]{3,2,1,0:T(8,128)(2,1)}, f32[12,128,6]{2,1,0:T(8,128)}, bf16[12,768,128]{2,...) while((s32[]{:T(128)}, bf16[80,128,640]{2,1,0:T(8,128)(2,1)}, ...), condition=%wide.region_1.2_spmd, body=%wide.region_0.1_spmd.sunk | while | flops 10 | bytes 798937 | solution.py:313
  338.0 1.5 dynamic-slice_bitcast_fusion.6
  339.5 1.8 dynamic-slice_bitcast_fusion.7
  341.4 429.2 %update.22 = (bf16[80,128,640]{2,1,0:T(8,128)(2,1)}, bf16[8,16,80,640]{3,2,1,0:T(8,128)(2,1)}, bf16[8,16,80,640]{3,2,1,0:T(8,128)(2,1)}, bf16[8,16,2,80,640]{4,3,2,1,0:T(8,128)(2,1)}) custom-call(bf16[80,128,640]{2,1,0:T(8,128)(2,1)} %get-tuple-element.275.refs_0_, bf16[8,16,80,640]{3,2,1,0:T(8,128)(2,1)} %get-tuple-element.276.refs_1_, ...), custom_call_target="tpu_custom_call" | custom-call | tf_op jit(solution)/shard_map/while/body/eval_jaxpr/update/pallas_call | solution.py:273
  770.5 429.0 %update.23 = (bf16[80,128,640]{2,1,0:T(8,128)(2,1)}, bf16[8,16,80,640]{3,2,1,0:T(8,128)(2,1)}, bf16[8,16,80,640]{3,2,1,0:T(8,128)(2,1)}, bf16[8,16,2,80,640]{4,3,2,1,0:T(8,128)(2,1)}) custom-call(bf16[80,128,640]{2,1,0:T(8,128)(2,1)} %get-tuple-element.257.refs_0_, bf16[8,16,80,640]{3,2,1,0:T(8,128)(2,1)} %get-tuple-element.258.refs_1_, ...), custom_call_target="tpu_custom_call" | custom-call | tf_op jit(solution)/shard_map/while/body/eval_jaxpr/update/pallas_call | solution.py:273
  1199.6 1.5 dynamic-slice_bitcast_fusion.6
  1201.1 1.8 dynamic-slice_bitcast_fusion.7
  1202.9 429.2 %update.22 = (bf16[80,128,640]{2,1,0:T(8,128)(2,1)}, bf16[8,16,80,640]{3,2,1,0:T(8,128)(2,1)}, bf16[8,16,80,640]{3,2,1,0:T(8,128)(2,1)}, bf16[8,16,2,80,640]{4,3,2,1,0:T(8,128)(2,1)}) custom-call(bf16[80,128,640]{2,1,0:T(8,128)(2,1)} %get-tuple-element.275.refs_0_, bf16[8,16,80,640]{3,2,1,0:T(8,128)(2,1)} %get-tuple-element.276.refs_1_, ...), custom_call_target="tpu_custom_call" | custom-call | tf_op jit(solution)/shard_map/while/body/eval_jaxpr/update/pallas_call | solution.py:273
  1632.2 429.0 %update.23 = (bf16[80,128,640]{2,1,0:T(8,128)(2,1)}, bf16[8,16,80,640]{3,2,1,0:T(8,128)(2,1)}, bf16[8,16,80,640]{3,2,1,0:T(8,128)(2,1)}, bf16[8,16,2,80,640]{4,3,2,1,0:T(8,128)(2,1)}) custom-call(bf16[80,128,640]{2,1,0:T(8,128)(2,1)} %get-tuple-element.257.refs_0_, bf16[8,16,80,640]{3,2,1,0:T(8,128)(2,1)} %get-tuple-element.258.refs_1_, ...), custom_call_target="tpu_custom_call" | custom-call | tf_op jit(solution)/shard_map/while/body/eval_jaxpr/update/pallas_call | solution.py:273
  2061.2 1.5 dynamic-slice_bitcast_fusion.6
  2062.7 1.8 dynamic-slice_bitcast_fusion.7
  2064.5 429.2 %update.22 = (bf16[80,128,640]{2,1,0:T(8,128)(2,1)}, bf16[8,16,80,640]{3,2,1,0:T(8,128)(2,1)}, bf16[8,16,80,640]{3,2,1,0:T(8,128)(2,1)}, bf16[8,16,2,80,640]{4,3,2,1,0:T(8,128)(2,1)}) custom-call(bf16[80,128,640]{2,1,0:T(8,128)(2,1)} %get-tuple-element.275.refs_0_, bf16[8,16,80,640]{3,2,1,0:T(8,128)(2,1)} %get-tuple-element.276.refs_1_, ...), custom_call_target="tpu_custom_call" | custom-call | tf_op jit(solution)/shard_map/while/body/eval_jaxpr/update/pallas_call | solution.py:273
  2493.8 429.0 %update.23 = (bf16[80,128,640]{2,1,0:T(8,128)(2,1)}, bf16[8,16,80,640]{3,2,1,0:T(8,128)(2,1)}, bf16[8,16,80,640]{3,2,1,0:T(8,128)(2,1)}, bf16[8,16,2,80,640]{4,3,2,1,0:T(8,128)(2,1)}) custom-call(bf16[80,128,640]{2,1,0:T(8,128)(2,1)} %get-tuple-element.257.refs_0_, bf16[8,16,80,640]{3,2,1,0:T(8,128)(2,1)} %get-tuple-element.258.refs_1_, ...), custom_call_target="tpu_custom_call" | custom-call | tf_op jit(solution)/shard_map/while/body/eval_jaxpr/update/pallas_call | solution.py:273
  2922.8 1.5 dynamic-slice_bitcast_fusion.6
  2924.3 1.8 dynamic-slice_bitcast_fusion.7
  2926.1 429.2 %update.22 = (bf16[80,128,640]{2,1,0:T(8,128)(2,1)}, bf16[8,16,80,640]{3,2,1,0:T(8,128)(2,1)}, bf16[8,16,80,640]{3,2,1,0:T(8,128)(2,1)}, bf16[8,16,2,80,640]{4,3,2,1,0:T(8,128)(2,1)}) custom-call(bf16[80,128,640]{2,1,0:T(8,128)(2,1)} %get-tuple-element.275.refs_0_, bf16[8,16,80,640]{3,2,1,0:T(8,128)(2,1)} %get-tuple-element.276.refs_1_, ...), custom_call_target="tpu_custom_call" | custom-call | tf_op jit(solution)/shard_map/while/body/eval_jaxpr/update/pallas_call | solution.py:273
  3355.4 429.0 %update.23 = (bf16[80,128,640]{2,1,0:T(8,128)(2,1)}, bf16[8,16,80,640]{3,2,1,0:T(8,128)(2,1)}, bf16[8,16,80,640]{3,2,1,0:T(8,128)(2,1)}, bf16[8,16,2,80,640]{4,3,2,1,0:T(8,128)(2,1)}) custom-call(bf16[80,128,640]{2,1,0:T(8,128)(2,1)} %get-tuple-element.257.refs_0_, bf16[8,16,80,640]{3,2,1,0:T(8,128)(2,1)} %get-tuple-element.258.refs_1_, ...), custom_call_target="tpu_custom_call" | custom-call | tf_op jit(solution)/shard_map/while/body/eval_jaxpr/update/pallas_call | solution.py:273
  3784.4 1.5 dynamic-slice_bitcast_fusion.6
  3786.0 1.8 dynamic-slice_bitcast_fusion.7
  3787.8 429.2 %update.22 = (bf16[80,128,640]{2,1,0:T(8,128)(2,1)}, bf16[8,16,80,640]{3,2,1,0:T(8,128)(2,1)}, bf16[8,16,80,640]{3,2,1,0:T(8,128)(2,1)}, bf16[8,16,2,80,640]{4,3,2,1,0:T(8,128)(2,1)}) custom-call(bf16[80,128,640]{2,1,0:T(8,128)(2,1)} %get-tuple-element.275.refs_0_, bf16[8,16,80,640]{3,2,1,0:T(8,128)(2,1)} %get-tuple-element.276.refs_1_, ...), custom_call_target="tpu_custom_call" | custom-call | tf_op jit(solution)/shard_map/while/body/eval_jaxpr/update/pallas_call | solution.py:273
  4217.0 429.0 %update.23 = (bf16[80,128,640]{2,1,0:T(8,128)(2,1)}, bf16[8,16,80,640]{3,2,1,0:T(8,128)(2,1)}, bf16[8,16,80,640]{3,2,1,0:T(8,128)(2,1)}, bf16[8,16,2,80,640]{4,3,2,1,0:T(8,128)(2,1)}) custom-call(bf16[80,128,640]{2,1,0:T(8,128)(2,1)} %get-tuple-element.257.refs_0_, bf16[8,16,80,640]{3,2,1,0:T(8,128)(2,1)} %get-tuple-element.258.refs_1_, ...), custom_call_target="tpu_custom_call" | custom-call | tf_op jit(solution)/shard_map/while/body/eval_jaxpr/update/pallas_call | solution.py:273
  4646.0 429.3 %update.20 = (bf16[80,128,640]{2,1,0:T(8,128)(2,1)}, bf16[8,16,80,640]{3,2,1,0:T(8,128)(2,1)}, bf16[8,16,80,640]{3,2,1,0:T(8,128)(2,1)}, bf16[8,16,2,80,640]{4,3,2,1,0:T(8,128)(2,1)}) custom-call(bf16[80,128,640]{2,1,0:T(8,128)(2,1)} %get-tuple-element.171.refs_0_, bf16[8,16,80,640]{3,2,1,0:T(8,128)(2,1)} %get-tuple-element.172.refs_1_, ...), custom_call_target="tpu_custom_call" | custom-call | tf_op jit(solution)/shard_map/update/pallas_call | solution.py:273
  5075.3 160.2 %update.21 = (bf16[80,128,640]{2,1,0:T(8,128)(2,1)}, bf16[8,16,80,640]{3,2,1,0:T(8,128)(2,1)}) custom-call(bf16[80,128,640]{2,1,0:T(8,128)(2,1)} %get-tuple-element.173.refs_0_, bf16[8,16,80,640]{3,2,1,0:T(8,128)(2,1)} %get-tuple-element.174.refs_1_, f32[128,6]{1,0:T(8,128)} %get-tuple-element.201.refs_2_, bf16[768,128]{1,0:T(8,128)(2,1)} %get-tuple-element.199.refs_3_), custom_call_target="tpu_custom_call" | custom-call | tf_op jit(solution)/shard_map/update/pallas_call | solution.py:273
  5235.5 17.5 copy.49
  (5 shorter events, 0.0 us)
Async XLA Ops:
  6.1 23.7 copy-start.1
  10.0 1.4 copy-start
